TPU v7x, 32 devices: a whole 2x2x4 slice. The times are simulated.
32 devices in a mesh: dp: 2 (over x), tp: 4 (over z), cp: 4 (over y, core).
Axes of the slice: x: 2, y: 2, z: 4, core: 2. Of those that a mesh axis runs over, the one named last changes fastest.
Arguments:
- x_in: bfloat16 [16384, 4096], P(('dp', 'cp')), parts along dimension 0
- positions: int32 [16384], P(('dp', 'cp')), parts along dimension 0
- norm_gain: bfloat16 [4096], replicated
- w_q: bfloat16 [4096, 4096], P(None, 'tp')
- w_k: bfloat16 [4096, 1024], P(None, 'tp')
- w_v: bfloat16 [4096, 1024], P(None, 'tp')
- w_o: bfloat16 [4096, 4096], P('tp')
Outputs:
- output 1: bfloat16 [16384, 4096], P(('dp', 'cp')), parts along dimension 0
- output 2: bfloat16 [16384, 8, 128], P(('dp', 'cp'), 'tp'), parts along dimension 0
- output 3: bfloat16 [16384, 8, 128], P(('dp', 'cp'), 'tp'), parts along dimension 0
There are 2 independent parts. A program takes and returns all parts, laid end to end along the dimension named above; an argument that names none is the same for every part.
All inputs are finite; a program needn't handle non-finite values.
Results may differ from a plain program's by a relative error of at most 0.00580332.
Values are sent between devices in bfloat16 or wider.
A program may use at most 1 GiB of HBM per device.

v0:
```python
import math
import jax
import jax.numpy as jnp
from jax import lax
from jax.sharding import PartitionSpec as P

HEAD_DIM = 128
NORM_EPS = 1e-5


def rope_freqs():
    exponent = jnp.arange(0, HEAD_DIM, 2).astype(jnp.float32) / HEAD_DIM
    base_freq = 1.0 / (500000.0 ** exponent)
    wave_len = 2.0 * math.pi / base_freq
    smooth = (8192.0 / wave_len - 1.0) / 3.0
    blended = (1.0 - smooth) * base_freq / 8.0 + smooth * base_freq
    return jnp.where(wave_len < 2048.0, base_freq, jnp.where(wave_len > 8192.0, base_freq / 8.0, blended))


def apply_rope(vecs, positions, freqs):
    half_dim = HEAD_DIM // 2
    angles = positions.astype(jnp.float32)[:, None] * freqs[None, :]
    cosine = jnp.cos(angles)[:, None, :]
    sine_val = jnp.sin(angles)[:, None, :]
    vec_f32 = vecs.astype(jnp.float32)
    first_half = vec_f32[..., :half_dim]
    second_half = vec_f32[..., half_dim:]
    return jnp.concatenate([first_half * cosine - second_half * sine_val, second_half * cosine + first_half * sine_val], axis=-1).astype(jnp.bfloat16)


def rms_norm(x_rows, norm_gain):
    x_f32 = x_rows.astype(jnp.float32)
    normed = x_f32 * lax.rsqrt(jnp.mean(x_f32 * x_f32, axis=-1, keepdims=True) + NORM_EPS)
    return (normed * norm_gain.astype(jnp.float32)[None, :]).astype(jnp.bfloat16)


def query_block(q_rows, key_rows, heads):
    blk_rows = q_rows
    while blk_rows % 2 == 0 and blk_rows > 8 and blk_rows * key_rows * heads > 2 ** 24:
        blk_rows = blk_rows // 2
    return blk_rows


def attend_all(queries, q_pos, keys, values, key_pos):
    q_rows = queries.shape[0]
    kv_heads = queries.shape[1]
    group_size = queries.shape[2]
    blk_rows = query_block(q_rows, keys.shape[0], kv_heads * group_size)
    n_blocks = q_rows // blk_rows
    q_blocks = queries.reshape(n_blocks, blk_rows, kv_heads, group_size, HEAD_DIM)
    pos_blocks = q_pos.reshape(n_blocks, blk_rows)
    score_scale = 1.0 / math.sqrt(HEAD_DIM)

    def one_block(block):
        q_part, pos_part = block
        scores = jnp.einsum('qhgd,thd->qhgt', q_part, keys, preferred_element_type=jnp.float32) * score_scale
        keep_mask = key_pos[None, None, None, :] <= pos_part[:, None, None, None]
        scores = jnp.where(keep_mask, scores, -jnp.inf)
        prob_bf = jax.nn.softmax(scores, axis=-1).astype(jnp.bfloat16)
        return jnp.einsum('qhgt,thd->qhgd', prob_bf, values, preferred_element_type=jnp.float32).astype(jnp.bfloat16)

    o_blocks = lax.map(one_block, (q_blocks, pos_blocks))
    return o_blocks.reshape(q_rows, kv_heads * group_size * HEAD_DIM)


def solution(mesh):
    n_tp = mesh.shape['tp']

    def device_fn(x_in, positions, norm_gain, w_q, w_k, w_v, w_o):
        local_rows = x_in.shape[0]
        heads_dev = w_q.shape[1] // HEAD_DIM
        kv_dev = w_k.shape[1] // HEAD_DIM
        group_size = heads_dev // kv_dev
        hidden = rms_norm(x_in, norm_gain)
        freqs = rope_freqs()
        queries = jnp.dot(hidden, w_q, preferred_element_type=jnp.float32).astype(jnp.bfloat16).reshape(local_rows, heads_dev, HEAD_DIM)
        keys = jnp.dot(hidden, w_k, preferred_element_type=jnp.float32).astype(jnp.bfloat16).reshape(local_rows, kv_dev, HEAD_DIM)
        values = jnp.dot(hidden, w_v, preferred_element_type=jnp.float32).astype(jnp.bfloat16).reshape(local_rows, kv_dev, HEAD_DIM)
        queries = apply_rope(queries, positions, freqs).reshape(local_rows, kv_dev, group_size, HEAD_DIM)
        keys = apply_rope(keys, positions, freqs)
        keys_all = lax.all_gather(keys, 'cp', axis=0, tiled=True)
        values_all = lax.all_gather(values, 'cp', axis=0, tiled=True)
        pos_all = lax.all_gather(positions, 'cp', axis=0, tiled=True)
        attn = attend_all(queries, positions, keys_all, values_all, pos_all)
        part_out = jnp.dot(attn, w_o, preferred_element_type=jnp.float32)
        summed = lax.psum_scatter(part_out, 'tp', scatter_dimension=0, tiled=True)
        share_rows = local_rows // n_tp
        x_share = lax.dynamic_slice_in_dim(x_in, lax.axis_index('tp') * share_rows, share_rows, axis=0)
        y_share = (x_share.astype(jnp.float32) + summed).astype(jnp.bfloat16)
        y_out = lax.all_gather(y_share, 'tp', axis=0, tiled=True)
        return y_out, keys, values

    row_spec = P(('dp', 'cp'), None)
    cache_spec = P(('dp', 'cp'), 'tp', None)
    return jax.shard_map(device_fn, mesh=mesh, in_specs=(row_spec, P(('dp', 'cp')), P(None), P(None, 'tp'), P(None, 'tp'), P(None, 'tp'), P('tp', None)), out_specs=(row_spec, cache_spec, cache_spec), check_vma=False)
```

profile of v0, /device:TPU:0, one launch (start us, length us, event | category | flops | bytes accessed | tf_op | source)
XLA Modules:
  0.0 2003.5 jit_solution(13521393403839303208)
XLA Ops:
  7.3 7.4 fusion.26
  14.7 8.7 convolution_convert_fusion.2
  23.4 1.2 fusion.33
  24.6 2.7 copy.46
  27.3 2.3 copy.47
  29.6 1.9 multiply_cosine_fusion
  31.5 1.3 copy.36
  32.8 1.3 copy.38
  34.1 6.1 subtract_convert_fusion.1
  40.3 3.7 pad_maximum_fusion.1
  44.2 9.3 convolution_convert_fusion.1
  53.5 1.4 copy.39
  55.0 23.7 %convolution_convert_fusion = bf16[2048,1024]{0,1:T(8,128)(2,1)S(1)} fusion(bf16[4096,1024]{1,0:T(8,128)(2,1)} %param.12, bf16[2048,4096]{1,0:T(8,128)(2,1)} %param.9, f32[4096]{0:T(1024)S(1)} %convert_element_type.61, f32[2048]{0:T(1024)S(1)} %add_rsqrt_fusion), kind=kOutput, calls=%fused_computation.33 | convolution fusion | flops 17215520768 | bytes 29384704 | tf_op jit(solution)/shard_map/dot_general | solution.py:76
  78.7 1.1 convert.20
  79.8 1.4 subtract_convert_fusion
  81.9 0.7 copy.49
  82.6 2.3 pad_maximum_fusion
  84.9 8.0 copy.40
  92.9 6.7 all_gather.12
  99.5 4.7 copy.41
  104.2 13.6 all-gather.6.cloned.1.call-done
  117.8 984.7 %while.10 = (s32[]{:T(128)}, bf16[8,256,2,4,128]{4,1,3,2,0:T(8,128)(2,1)}, s32[8192]{0:T(1024)S(1)}, s32[8,256]{1,0:T(8,128)S(1)}, bf16[8,256,2,4,128]{4,1,3,2,0...) while((s32[]{:T(128)}, ...), condition=%wide.region_4.5_spmd, body=%wide.region_1.4_spmd.sunk | while | flops 8726519808 | bytes 298897536 | solution.py:62
  117.8 26.5 %fusion.49 = f32[2,256,4,8192]{3,1,2,0:T(8,128)} fusion(bf16[8192,2,128]{2,0,1:T(8,128)(2,1)} %get-tuple-element.173, bf16[8,256,2,4,128]{4,1,3,2,0:T(8,128)(2,1)} %get-tuple-element.172, s32[]{:T(128)} %get-tuple-element.160), kind=kOutput, calls=%fused_computation.12.clone.1 | convolution fusion | flops 4294967296 | bytes 71827968 | tf_op jit(solution)/shard_map/while/body/eval_jaxpr/qhgd,thd->qhgt/dot_general | solution.py:56
  144.3 1.2 broadcast_compare_fusion.2
  145.5 71.7 %fusion.50 = (f32[256,2,4]{0,2,1:T(4,128)S(1)}, f32[256,2,4,8192]{3,0,2,1:T(8,128)}) fusion(f32[2,256,4,8192]{3,1,2,0:T(8,128)} %fusion.49, pred[256,8192]{1,0:T(8,128)(4,1)S(1)} %broadcast_compare_fusion.2), kind=kOutput, calls=%fused_computation.44.clone.1 | output fusion | flops 100671488 | bytes 136323072 | tf_op jit(solution)/shard_map/while/body/eval_jaxpr/sub | solution.py:59
  217.3 23.6 %fusion.51 = bf16[8,256,2,4,128]{4,1,3,2,0:T(8,128)(2,1)} fusion(bf16[8,256,2,4,128]{4,1,3,2,0:T(8,128)(2,1)} %get-tuple-element.161, s32[]{:T(128)} %get-tuple-element.160, bf16[8192,2,128]{2,0,1:T(8,128)(2,1)S(1)} %copy-done.7, f32[256,2,4,8192]{3,0,2,1:T(8,128)} %get-tuple-element.150, f32[256,2,4]{0,2,1:T(4,128)S(1)} %get-tuple-element.151), kind=kOutput, calls=%fused_computation.17.clone.1 | convolution fusion | flops 4328783872 | bytes 71836160 | tf_op jit(solution)/shard_map/while/body/eval_jaxpr/qhgt,thd->qhgd/dot_general | solution.py:60
  240.9 26.5 %fusion.49 = f32[2,256,4,8192]{3,1,2,0:T(8,128)} fusion(bf16[8192,2,128]{2,0,1:T(8,128)(2,1)} %get-tuple-element.173, bf16[8,256,2,4,128]{4,1,3,2,0:T(8,128)(2,1)} %get-tuple-element.172, s32[]{:T(128)} %get-tuple-element.160), kind=kOutput, calls=%fused_computation.12.clone.1 | convolution fusion | flops 4294967296 | bytes 71827968 | tf_op jit(solution)/shard_map/while/body/eval_jaxpr/qhgd,thd->qhgt/dot_general | solution.py:56
  267.4 1.2 broadcast_compare_fusion.2
  268.6 71.7 %fusion.50 = (f32[256,2,4]{0,2,1:T(4,128)S(1)}, f32[256,2,4,8192]{3,0,2,1:T(8,128)}) fusion(f32[2,256,4,8192]{3,1,2,0:T(8,128)} %fusion.49, pred[256,8192]{1,0:T(8,128)(4,1)S(1)} %broadcast_compare_fusion.2), kind=kOutput, calls=%fused_computation.44.clone.1 | output fusion | flops 100671488 | bytes 136323072 | tf_op jit(solution)/shard_map/while/body/eval_jaxpr/sub | solution.py:59
  340.4 23.6 %fusion.51 = bf16[8,256,2,4,128]{4,1,3,2,0:T(8,128)(2,1)} fusion(bf16[8,256,2,4,128]{4,1,3,2,0:T(8,128)(2,1)} %get-tuple-element.161, s32[]{:T(128)} %get-tuple-element.160, bf16[8192,2,128]{2,0,1:T(8,128)(2,1)S(1)} %copy-done.7, f32[256,2,4,8192]{3,0,2,1:T(8,128)} %get-tuple-element.150, f32[256,2,4]{0,2,1:T(4,128)S(1)} %get-tuple-element.151), kind=kOutput, calls=%fused_computation.17.clone.1 | convolution fusion | flops 4328783872 | bytes 71836160 | tf_op jit(solution)/shard_map/while/body/eval_jaxpr/qhgt,thd->qhgd/dot_general | solution.py:60
  364.0 26.5 %fusion.49 = f32[2,256,4,8192]{3,1,2,0:T(8,128)} fusion(bf16[8192,2,128]{2,0,1:T(8,128)(2,1)} %get-tuple-element.173, bf16[8,256,2,4,128]{4,1,3,2,0:T(8,128)(2,1)} %get-tuple-element.172, s32[]{:T(128)} %get-tuple-element.160), kind=kOutput, calls=%fused_computation.12.clone.1 | convolution fusion | flops 4294967296 | bytes 71827968 | tf_op jit(solution)/shard_map/while/body/eval_jaxpr/qhgd,thd->qhgt/dot_general | solution.py:56
  390.5 1.2 broadcast_compare_fusion.2
  391.7 71.7 %fusion.50 = (f32[256,2,4]{0,2,1:T(4,128)S(1)}, f32[256,2,4,8192]{3,0,2,1:T(8,128)}) fusion(f32[2,256,4,8192]{3,1,2,0:T(8,128)} %fusion.49, pred[256,8192]{1,0:T(8,128)(4,1)S(1)} %broadcast_compare_fusion.2), kind=kOutput, calls=%fused_computation.44.clone.1 | output fusion | flops 100671488 | bytes 136323072 | tf_op jit(solution)/shard_map/while/body/eval_jaxpr/sub | solution.py:59
  463.5 23.6 %fusion.51 = bf16[8,256,2,4,128]{4,1,3,2,0:T(8,128)(2,1)} fusion(bf16[8,256,2,4,128]{4,1,3,2,0:T(8,128)(2,1)} %get-tuple-element.161, s32[]{:T(128)} %get-tuple-element.160, bf16[8192,2,128]{2,0,1:T(8,128)(2,1)S(1)} %copy-done.7, f32[256,2,4,8192]{3,0,2,1:T(8,128)} %get-tuple-element.150, f32[256,2,4]{0,2,1:T(4,128)S(1)} %get-tuple-element.151), kind=kOutput, calls=%fused_computation.17.clone.1 | convolution fusion | flops 4328783872 | bytes 71836160 | tf_op jit(solution)/shard_map/while/body/eval_jaxpr/qhgt,thd->qhgd/dot_general | solution.py:60
  487.1 26.4 %fusion.49 = f32[2,256,4,8192]{3,1,2,0:T(8,128)} fusion(bf16[8192,2,128]{2,0,1:T(8,128)(2,1)} %get-tuple-element.173, bf16[8,256,2,4,128]{4,1,3,2,0:T(8,128)(2,1)} %get-tuple-element.172, s32[]{:T(128)} %get-tuple-element.160), kind=kOutput, calls=%fused_computation.12.clone.1 | convolution fusion | flops 4294967296 | bytes 71827968 | tf_op jit(solution)/shard_map/while/body/eval_jaxpr/qhgd,thd->qhgt/dot_general | solution.py:56
  513.6 1.2 broadcast_compare_fusion.2
  514.8 71.7 %fusion.50 = (f32[256,2,4]{0,2,1:T(4,128)S(1)}, f32[256,2,4,8192]{3,0,2,1:T(8,128)}) fusion(f32[2,256,4,8192]{3,1,2,0:T(8,128)} %fusion.49, pred[256,8192]{1,0:T(8,128)(4,1)S(1)} %broadcast_compare_fusion.2), kind=kOutput, calls=%fused_computation.44.clone.1 | output fusion | flops 100671488 | bytes 136323072 | tf_op jit(solution)/shard_map/while/body/eval_jaxpr/sub | solution.py:59
  586.5 23.6 %fusion.51 = bf16[8,256,2,4,128]{4,1,3,2,0:T(8,128)(2,1)} fusion(bf16[8,256,2,4,128]{4,1,3,2,0:T(8,128)(2,1)} %get-tuple-element.161, s32[]{:T(128)} %get-tuple-element.160, bf16[8192,2,128]{2,0,1:T(8,128)(2,1)S(1)} %copy-done.7, f32[256,2,4,8192]{3,0,2,1:T(8,128)} %get-tuple-element.150, f32[256,2,4]{0,2,1:T(4,128)S(1)} %get-tuple-element.151), kind=kOutput, calls=%fused_computation.17.clone.1 | convolution fusion | flops 4328783872 | bytes 71836160 | tf_op jit(solution)/shard_map/while/body/eval_jaxpr/qhgt,thd->qhgd/dot_general | solution.py:60
  610.2 26.4 %fusion.49 = f32[2,256,4,8192]{3,1,2,0:T(8,128)} fusion(bf16[8192,2,128]{2,0,1:T(8,128)(2,1)} %get-tuple-element.173, bf16[8,256,2,4,128]{4,1,3,2,0:T(8,128)(2,1)} %get-tuple-element.172, s32[]{:T(128)} %get-tuple-element.160), kind=kOutput, calls=%fused_computation.12.clone.1 | convolution fusion | flops 4294967296 | bytes 71827968 | tf_op jit(solution)/shard_map/while/body/eval_jaxpr/qhgd,thd->qhgt/dot_general | solution.py:56
  636.6 1.2 broadcast_compare_fusion.2
  637.9 71.7 %fusion.50 = (f32[256,2,4]{0,2,1:T(4,128)S(1)}, f32[256,2,4,8192]{3,0,2,1:T(8,128)}) fusion(f32[2,256,4,8192]{3,1,2,0:T(8,128)} %fusion.49, pred[256,8192]{1,0:T(8,128)(4,1)S(1)} %broadcast_compare_fusion.2), kind=kOutput, calls=%fused_computation.44.clone.1 | output fusion | flops 100671488 | bytes 136323072 | tf_op jit(solution)/shard_map/while/body/eval_jaxpr/sub | solution.py:59
  709.6 23.6 %fusion.51 = bf16[8,256,2,4,128]{4,1,3,2,0:T(8,128)(2,1)} fusion(bf16[8,256,2,4,128]{4,1,3,2,0:T(8,128)(2,1)} %get-tuple-element.161, s32[]{:T(128)} %get-tuple-element.160, bf16[8192,2,128]{2,0,1:T(8,128)(2,1)S(1)} %copy-done.7, f32[256,2,4,8192]{3,0,2,1:T(8,128)} %get-tuple-element.150, f32[256,2,4]{0,2,1:T(4,128)S(1)} %get-tuple-element.151), kind=kOutput, calls=%fused_computation.17.clone.1 | convolution fusion | flops 4328783872 | bytes 71836160 | tf_op jit(solution)/shard_map/while/body/eval_jaxpr/qhgt,thd->qhgd/dot_general | solution.py:60
  733.3 26.5 %fusion.49 = f32[2,256,4,8192]{3,1,2,0:T(8,128)} fusion(bf16[8192,2,128]{2,0,1:T(8,128)(2,1)} %get-tuple-element.173, bf16[8,256,2,4,128]{4,1,3,2,0:T(8,128)(2,1)} %get-tuple-element.172, s32[]{:T(128)} %get-tuple-element.160), kind=kOutput, calls=%fused_computation.12.clone.1 | convolution fusion | flops 4294967296 | bytes 71827968 | tf_op jit(solution)/shard_map/while/body/eval_jaxpr/qhgd,thd->qhgt/dot_general | solution.py:56
  759.7 1.2 broadcast_compare_fusion.2
  761.0 71.7 %fusion.50 = (f32[256,2,4]{0,2,1:T(4,128)S(1)}, f32[256,2,4,8192]{3,0,2,1:T(8,128)}) fusion(f32[2,256,4,8192]{3,1,2,0:T(8,128)} %fusion.49, pred[256,8192]{1,0:T(8,128)(4,1)S(1)} %broadcast_compare_fusion.2), kind=kOutput, calls=%fused_computation.44.clone.1 | output fusion | flops 100671488 | bytes 136323072 | tf_op jit(solution)/shard_map/while/body/eval_jaxpr/sub | solution.py:59
  832.7 23.6 %fusion.51 = bf16[8,256,2,4,128]{4,1,3,2,0:T(8,128)(2,1)} fusion(bf16[8,256,2,4,128]{4,1,3,2,0:T(8,128)(2,1)} %get-tuple-element.161, s32[]{:T(128)} %get-tuple-element.160, bf16[8192,2,128]{2,0,1:T(8,128)(2,1)S(1)} %copy-done.7, f32[256,2,4,8192]{3,0,2,1:T(8,128)} %get-tuple-element.150, f32[256,2,4]{0,2,1:T(4,128)S(1)} %get-tuple-element.151), kind=kOutput, calls=%fused_computation.17.clone.1 | convolution fusion | flops 4328783872 | bytes 71836160 | tf_op jit(solution)/shard_map/while/body/eval_jaxpr/qhgt,thd->qhgd/dot_general | solution.py:60
  856.3 26.5 %fusion.49 = f32[2,256,4,8192]{3,1,2,0:T(8,128)} fusion(bf16[8192,2,128]{2,0,1:T(8,128)(2,1)} %get-tuple-element.173, bf16[8,256,2,4,128]{4,1,3,2,0:T(8,128)(2,1)} %get-tuple-element.172, s32[]{:T(128)} %get-tuple-element.160), kind=kOutput, calls=%fused_computation.12.clone.1 | convolution fusion | flops 4294967296 | bytes 71827968 | tf_op jit(solution)/shard_map/while/body/eval_jaxpr/qhgd,thd->qhgt/dot_general | solution.py:56
  882.8 1.2 broadcast_compare_fusion.2
  884.0 71.7 %fusion.50 = (f32[256,2,4]{0,2,1:T(4,128)S(1)}, f32[256,2,4,8192]{3,0,2,1:T(8,128)}) fusion(f32[2,256,4,8192]{3,1,2,0:T(8,128)} %fusion.49, pred[256,8192]{1,0:T(8,128)(4,1)S(1)} %broadcast_compare_fusion.2), kind=kOutput, calls=%fused_computation.44.clone.1 | output fusion | flops 100671488 | bytes 136323072 | tf_op jit(solution)/shard_map/while/body/eval_jaxpr/sub | solution.py:59
  955.8 23.6 %fusion.51 = bf16[8,256,2,4,128]{4,1,3,2,0:T(8,128)(2,1)} fusion(bf16[8,256,2,4,128]{4,1,3,2,0:T(8,128)(2,1)} %get-tuple-element.161, s32[]{:T(128)} %get-tuple-element.160, bf16[8192,2,128]{2,0,1:T(8,128)(2,1)S(1)} %copy-done.7, f32[256,2,4,8192]{3,0,2,1:T(8,128)} %get-tuple-element.150, f32[256,2,4]{0,2,1:T(4,128)S(1)} %get-tuple-element.151), kind=kOutput, calls=%fused_computation.17.clone.1 | convolution fusion | flops 4328783872 | bytes 71836160 | tf_op jit(solution)/shard_map/while/body/eval_jaxpr/qhgt,thd->qhgd/dot_general | solution.py:60
  979.4 26.5 %fusion.49 = f32[2,256,4,8192]{3,1,2,0:T(8,128)} fusion(bf16[8192,2,128]{2,0,1:T(8,128)(2,1)} %get-tuple-element.173, bf16[8,256,2,4,128]{4,1,3,2,0:T(8,128)(2,1)} %get-tuple-element.172, s32[]{:T(128)} %get-tuple-element.160), kind=kOutput, calls=%fused_computation.12.clone.1 | convolution fusion | flops 4294967296 | bytes 71827968 | tf_op jit(solution)/shard_map/while/body/eval_jaxpr/qhgd,thd->qhgt/dot_general | solution.py:56
  1005.9 1.2 broadcast_compare_fusion.2
  1007.1 71.7 %fusion.50 = (f32[256,2,4]{0,2,1:T(4,128)S(1)}, f32[256,2,4,8192]{3,0,2,1:T(8,128)}) fusion(f32[2,256,4,8192]{3,1,2,0:T(8,128)} %fusion.49, pred[256,8192]{1,0:T(8,128)(4,1)S(1)} %broadcast_compare_fusion.2), kind=kOutput, calls=%fused_computation.44.clone.1 | output fusion | flops 100671488 | bytes 136323072 | tf_op jit(solution)/shard_map/while/body/eval_jaxpr/sub | solution.py:59
  1078.9 23.6 %fusion.51 = bf16[8,256,2,4,128]{4,1,3,2,0:T(8,128)(2,1)} fusion(bf16[8,256,2,4,128]{4,1,3,2,0:T(8,128)(2,1)} %get-tuple-element.161, s32[]{:T(128)} %get-tuple-element.160, bf16[8192,2,128]{2,0,1:T(8,128)(2,1)S(1)} %copy-done.7, f32[256,2,4,8192]{3,0,2,1:T(8,128)} %get-tuple-element.150, f32[256,2,4]{0,2,1:T(4,128)S(1)} %get-tuple-element.151), kind=kOutput, calls=%fused_computation.17.clone.1 | convolution fusion | flops 4328783872 | bytes 71836160 | tf_op jit(solution)/shard_map/while/body/eval_jaxpr/qhgt,thd->qhgd/dot_general | solution.py:60
  1102.5 7.8 copy.42
  1110.4 3.9 copy.50
  1114.2 0.8 copy-done.6
  1115.0 21.8 %fusion.34 = f32[2048,4096]{1,0:T(8,128)} fusion(bf16[2048,1024]{0,1:T(8,128)(2,1)S(1)} %bitcast.82, bf16[1024,4096]{1,0:T(8,128)(2,1)S(1)} %copy-done.6), kind=kOutput, calls=%fused_computation.46 | convolution fusion | flops 17179869184 | bytes 46137344 | tf_op jit(solution)/shard_map/dot_general | solution.py:85
  1136.9 549.3 %reduce-scatter.2.cloned.1.call-done = f32[512,4096]{1,0:T(8,128)} async-done(((f32[2048,4096]{1,0:T(8,128)}), f32[512,4096]{1,0:T(8,128)}) %reduce-scatter.2.cloned.1.call-update) | async-done | bytes 8388624 | tf_op jit(solution)/shard_map/reduce_scatter | solution.py:86
  1686.2 8.0 add_convert_fusion
  1694.2 1.2 copy-done.3
  1695.4 2.0 copy.43
  1697.4 284.9 %all-gather.8.cloned.1.call-done = bf16[2048,4096]{1,0:T(8,128)(2,1)} async-done(((bf16[512,4096]{1,0:T(8,128)(2,1)}), bf16[2048,4096]{1,0:T(8,128)(2,1)}) %all-gather.8.cloned.1.call-update) | async-done | bytes 16777232 | tf_op jit(solution)/shard_map/all_gather | solution.py:90
  1982.3 14.2 copy.59
  (52 shorter events, 1.2 us)
Async XLA Ops:
  7.2 7.5 copy-start
  7.2 92.4 %all-gather.4.cloned.1.call-start = ((), (), s32[]{:S(2)}) async-start(), calls=%async_computation.1 | async-start | bytes 5242880 | tf_op jit(solution)/shard_map/all_gather | solution.py:81
  7.2 7.4 copy-start.5
  24.6 5.0 copy-start.4
  44.0 73.9 %all-gather.6.cloned.1.call-start = ((), (), s32[]{:S(2)}) async-start(), calls=%async_computation.2 | async-start | bytes 5242880 | tf_op jit(solution)/shard_map/all_gather | solution.py:82
  53.5 25.2 %copy-start.2 = (bf16[2048,256]{0,1:T(8,128)(2,1)}, bf16[2048,256]{0,1:T(8,128)(2,1)S(1)}, u32[]{:S(2)}) copy-start(bf16[2048,256]{0,1:T(8,128)(2,1)S(1)} %convolution_convert_fusion.1) | copy-start | bytes 3145732
  54.9 1631.3 %reduce-scatter.2.cloned.1.call-start = ((), (), s32[]{:S(2)}) async-start(), calls=%async_computation.3 | async-start | bytes 41943040 | tf_op jit(solution)/shard_map/reduce_scatter | solution.py:86
  145.5 71.8 %copy-start.7 = (bf16[8192,2,128]{2,0,1:T(8,128)(2,1)S(1)}, bf16[8192,2,128]{2,0,1:T(8,128)(2,1)}, u32[]{:S(2)}) copy-start(bf16[8192,2,128]{2,0,1:T(8,128)(2,1)} %get-tuple-element.174) | copy-start | bytes 12582916 | tf_op jit(solution)/shard_map/while
  268.6 71.8 %copy-start.7 = (bf16[8192,2,128]{2,0,1:T(8,128)(2,1)S(1)}, bf16[8192,2,128]{2,0,1:T(8,128)(2,1)}, u32[]{:S(2)}) copy-start(bf16[8192,2,128]{2,0,1:T(8,128)(2,1)} %get-tuple-element.174) | copy-start | bytes 12582916 | tf_op jit(solution)/shard_map/while
  391.7 71.8 %copy-start.7 = (bf16[8192,2,128]{2,0,1:T(8,128)(2,1)S(1)}, bf16[8192,2,128]{2,0,1:T(8,128)(2,1)}, u32[]{:S(2)}) copy-start(bf16[8192,2,128]{2,0,1:T(8,128)(2,1)} %get-tuple-element.174) | copy-start | bytes 12582916 | tf_op jit(solution)/shard_map/while
  514.8 71.8 %copy-start.7 = (bf16[8192,2,128]{2,0,1:T(8,128)(2,1)S(1)}, bf16[8192,2,128]{2,0,1:T(8,128)(2,1)}, u32[]{:S(2)}) copy-start(bf16[8192,2,128]{2,0,1:T(8,128)(2,1)} %get-tuple-element.174) | copy-start | bytes 12582916 | tf_op jit(solution)/shard_map/while
  637.9 71.8 %copy-start.7 = (bf16[8192,2,128]{2,0,1:T(8,128)(2,1)S(1)}, bf16[8192,2,128]{2,0,1:T(8,128)(2,1)}, u32[]{:S(2)}) copy-start(bf16[8192,2,128]{2,0,1:T(8,128)(2,1)} %get-tuple-element.174) | copy-start | bytes 12582916 | tf_op jit(solution)/shard_map/while
  760.9 71.8 %copy-start.7 = (bf16[8192,2,128]{2,0,1:T(8,128)(2,1)S(1)}, bf16[8192,2,128]{2,0,1:T(8,128)(2,1)}, u32[]{:S(2)}) copy-start(bf16[8192,2,128]{2,0,1:T(8,128)(2,1)} %get-tuple-element.174) | copy-start | bytes 12582916 | tf_op jit(solution)/shard_map/while
  884.0 71.8 %copy-start.7 = (bf16[8192,2,128]{2,0,1:T(8,128)(2,1)S(1)}, bf16[8192,2,128]{2,0,1:T(8,128)(2,1)}, u32[]{:S(2)}) copy-start(bf16[8192,2,128]{2,0,1:T(8,128)(2,1)} %get-tuple-element.174) | copy-start | bytes 12582916 | tf_op jit(solution)/shard_map/while
  1007.1 71.8 %copy-start.7 = (bf16[8192,2,128]{2,0,1:T(8,128)(2,1)S(1)}, bf16[8192,2,128]{2,0,1:T(8,128)(2,1)}, u32[]{:S(2)}) copy-start(bf16[8192,2,128]{2,0,1:T(8,128)(2,1)} %get-tuple-element.174) | copy-start | bytes 12582916 | tf_op jit(solution)/shard_map/while
  1110.4 4.6 copy-start.6
  1136.9 845.5 %all-gather.8.cloned.1.call-start = ((), (), s32[]{:S(2)}) async-start(), calls=%async_computation.4 | async-start | bytes 20971520 | tf_op jit(solution)/shard_map/all_gather | solution.py:90
  1694.2 1.2 copy-start.3
  1982.3 14.2 copy-start.1
Sparse Core Ops, SparseCore 0:
  44.1 37.0 all-gather.3
  83.3 34.4 all-gather.5
  1137.0 549.1 reduce-scatter.1
  1694.3 287.9 all-gather.7
where the time goes:
time: 2010 us; the launch traced here: 2000 us
  waiting for transfers between devices  848 us (42%)
  other arithmetic  616 us (31%)
  matrix products  464 us (23%)
  local copies, waits for them, and re-layouts  54.1 us (3%)
    sub x8, other arithmetic, one_block(): prob_bf = jax.nn.softmax(scores, axis=-1).astype(jnp.bfloat16)  574 us
    reduce_scatter x1, waiting for transfers between devices, device_fn(): summed = lax.psum_scatter(part_out, 'tp', scatter_dimension=0, tiled=True)  549 us
    all_gather x1, waiting for transfers between devices, device_fn(): y_out = lax.all_gather(y_share, 'tp', axis=0, tiled=True)  285 us
    dot_general x8, matrix products, one_block(): jnp.einsum('qhgd,thd->qhgt', q_part, keys, preferred_element_type=jnp.flo...  212 us
    dot_general x8, matrix products, one_block(): jnp.einsum('qhgt,thd->qhgd', prob_bf, values, preferred_element_type=jnp....  189 us
  transfers between devices with their start and end apart: 4, of which 3 were waited for; matrix products, arithmetic and copies ran while one was open for 3% of the time, Pallas kernels for 0%

commit v1 on v0

v1 whole, which is shorter than its diff:
```python
import math
import jax
import jax.numpy as jnp
from jax import lax
from jax.experimental import pallas as pl
from jax.experimental.pallas import tpu as pltpu
from jax.sharding import PartitionSpec as P

HEAD_DIM = 128
NORM_EPS = 1e-5
NEG = -0.7 * float(jnp.finfo(jnp.float32).max)
SCALE2 = (1.0 / math.sqrt(HEAD_DIM)) * math.log2(math.e)
BF16 = jnp.bfloat16
F32 = jnp.float32
MESH = pl.DeviceIdType.MESH


def rope_freqs():
    exponent = jnp.arange(0, HEAD_DIM, 2).astype(jnp.float32) / HEAD_DIM
    base_freq = 1.0 / (500000.0 ** exponent)
    wave_len = 2.0 * math.pi / base_freq
    smooth = (8192.0 / wave_len - 1.0) / 3.0
    blended = (1.0 - smooth) * base_freq / 8.0 + smooth * base_freq
    return jnp.where(wave_len < 2048.0, base_freq, jnp.where(wave_len > 8192.0, base_freq / 8.0, blended))


def rotate(vec_bf, cos, sin):
    vec = vec_bf.astype(F32)
    return (vec * cos + pltpu.roll(vec, HEAD_DIM // 2, axis=1) * sin).astype(BF16)


def layer(x, gain, w_q, w_k, w_v, w_o, positions, freqs):
    rows, width = x.shape
    seg = rows // 2
    d = HEAD_DIM
    kvh = w_k.shape[1] // d
    group = w_q.shape[1] // w_k.shape[1]
    gw = group * d
    qw = kvh * gw
    n_tp = width // qw
    n_seg = 8
    total = n_seg * seg
    blk = 256
    n_blk = rows // blk
    half_w = width // 2
    bq, bk = 256, 512
    cols = bq * group
    unit_rows = 2 * bq
    slice_rows = qw // 8
    y_cols = 512
    nr = 32

    def kernel(x_ref, gain_ref, wq_ref, wk_ref, wv_ref, wo_ref, pos_ref, freq_ref,
               y_ref, k_ref, v_ref, oall_ref, wall_ref,
               big, kb, vb, qb, xb, csb, vst, qt, s_a, s_b, acc_a, acc_b, m_run, l_run, m_tile, yb,
               ld_sem, x_sem, vst_sem, kout_sem,
               kv_s, kv_r, wz_s, wz_r, wp_s, wp_r, wc_s, wc_r,
               o_s, o_l, o_r, f_s, ob_sem, yb_sem, wl_sem):
        dp, z, cp = lax.axis_index("dp"), lax.axis_index("tp"), lax.axis_index("cp")
        cy, cc = cp // 2, cp % 2
        x_nb = {"dp": 1 - dp}
        y_nb = {"cp": (1 - cy) * 2 + cc}
        c_nb = {"cp": cy * 2 + 1 - cc}
        peer = lambda off: {"tp": lax.rem(z + off, n_tp)}

        def remote(src, dst, ss, rs, dev):
            return pltpu.make_async_remote_copy(src_ref=src, dst_ref=dst, send_sem=ss, recv_sem=rs, device_id=dev, device_id_type=MESH)

        def got(region, rs):
            remote(region, region, rs, rs, x_nb).wait_recv()

        barrier = pltpu.get_barrier_semaphore()
        for dev in (x_nb, y_nb, c_nb, peer(1), peer(2), peer(3)):
            pl.semaphore_signal(barrier, inc=1, device_id=dev, device_id_type=MESH)
        pl.semaphore_wait(barrier, 6)

        place = dp * 4 + cp

        def w_rows(zs, fx, fy, fc):
            px = 1 - dp if fx else dp
            py = 1 - cy if fy else cy
            pc = 1 - cc if fc else cc
            return pl.multiple_of(zs * qw + (px * 4 + py * 2 + pc) * slice_rows, slice_rows)

        def w_piece(zs, fx, fy, fc, lo=0, n=slice_rows):
            return wall_ref.at[pl.ds(pl.multiple_of(w_rows(zs, fx, fy, fc) + lo, 64), n), :]

        middle = (z == 1) | (z == 2)
        partner = z + 1 - 2 * (z % 2)
        other_mid = jnp.where(z < 2, 2, 1)
        other_end = jnp.where(z < 2, 3, 0)
        sources = (z, partner, other_mid, other_end)
        slot_out = jnp.where(middle, 1, 2)

        src_z = lambda o: sources[o + 1]

        def z_copy(o):
            src = wo_ref.at[pl.ds(pl.multiple_of(place * slice_rows, slice_rows), slice_rows), :]
            dst = w_piece(z, 0, 0, 0)
            return remote(src, dst, wz_s.at[o], wz_r.at[0 if o == 0 else slot_out], {"tp": sources[o + 1]})

        def z_forward():
            there = w_piece(other_end, 0, 0, 0)
            return remote(there, there, wz_s.at[3], wz_r.at[2], {"tp": partner})
        half_n = slice_rows // 2

        def w_send(kind, o):
            zs = src_z(o)
            if kind == 0:
                return remote(w_piece(zs, 0, 0, 0), w_piece(zs, 0, 0, 0), wp_s.at[0, o], wp_r.at[0, o], x_nb)
            if kind == 1:
                return remote(w_piece(zs, 0, 0, 0), w_piece(zs, 0, 0, 0), wp_s.at[1, o], wp_r.at[1, o], y_nb)
            if kind == 2:
                return remote(w_piece(zs, 1, 0, 0, 0, half_n), w_piece(zs, 1, 0, 0, 0, half_n), wp_s.at[2, o], wp_r.at[2, o], y_nb)
            return remote(w_piece(zs, 0, 1, 0, half_n, half_n), w_piece(zs, 0, 1, 0, half_n, half_n), wp_s.at[3, o], wp_r.at[3, o], x_nb)

        def c_send(i, o):
            zs = src_z(o)
            piece = w_piece(zs, i & 1, i >> 1, 0)
            return remote(piece, piece, wc_s.at[i, o], wc_r.at[i, o], c_nb)

        def w_stage1(o):
            zs = src_z(o)
            if o < 2:
                got(w_piece(zs, 0, 0, 0), wz_r.at[o])
            else:
                @pl.when(jnp.logical_not(middle))
                def _():
                    got(w_piece(zs, 0, 0, 0), wz_r.at[o])

            w_send(0, o).start()
            w_send(1, o).start()
            c_send(0, o).start()

        def w_stage2(o):
            zs = src_z(o)
            got(w_piece(zs, 1, 0, 0), wp_r.at[0, o])
            w_send(2, o).start()
            c_send(1, o).start()
            got(w_piece(zs, 0, 1, 0), wp_r.at[1, o])
            w_send(3, o).start()
            c_send(2, o).start()

        def w_stage3(o):
            zs = src_z(o)
            got(w_piece(zs, 1, 1, 0, 0, half_n), wp_r.at[2, o])
            got(w_piece(zs, 1, 1, 0, half_n, half_n), wp_r.at[3, o])
            c_send(3, o).start()

        def w_load(zs, src, i):
            out = []
            for n in range(2):
                out.append(pltpu.make_async_copy(
                    src.at[:, pl.ds(n * half_w, half_w)],
                    big.at[n, pl.ds(pl.multiple_of(zs * qw, qw), qw), :], wl_sem.at[i, n]))
            return out

        def w_load_own():
            return w_load(z, wo_ref, 3)

        def w_load_other(o):
            zs = src_z(o)
            return w_load(zs, wall_ref.at[pl.ds(pl.multiple_of(zs * qw, qw), qw), :], o)

        def w_stage4(o):
            zs = src_z(o)
            for i in range(4):
                got(w_piece(zs, i & 1, i >> 1, 1), wc_r.at[i, o])
            for c in w_load_other(o):
                c.start()

        load_k = pltpu.make_async_copy(wk_ref, big.at[0, :, pl.ds(qw, kvh * d)], ld_sem.at[0])
        load_v = pltpu.make_async_copy(wv_ref, big.at[0, :, pl.ds(qw + kvh * d, kvh * d)], ld_sem.at[1])
        load_q = pltpu.make_async_copy(wq_ref, big.at[0, :, pl.ds(0, qw)], ld_sem.at[2])

        def x_copy(b, slot):
            return pltpu.make_async_copy(x_ref.at[pl.ds(pl.multiple_of(b * blk, blk), blk), :], xb.at[slot], x_sem.at[slot])

        low_lanes = lax.broadcasted_iota(jnp.int32, (blk, d), 1) < d // 2

        def make_angles(b):
            first = pos_ref[b * blk]
            pos = (lax.broadcasted_iota(jnp.int32, (blk, d), 0) + first).astype(F32)
            angle = pos * freq_ref[...]
            csb[pl.ds(pl.multiple_of(b * blk, blk), blk), :] = jnp.where(low_lanes, jnp.cos(angle), jnp.sin(angle))

        def cos_sin(b):
            both = csb[pl.ds(pl.multiple_of(b * blk, blk), blk), :]
            turned = pltpu.roll(both, d // 2, axis=1)
            return jnp.where(low_lanes, both, turned), jnp.where(low_lanes, -turned, both)

        def v_copy(b, slot):
            return pltpu.make_async_copy(vst.at[slot], v_ref.at[pl.ds(pl.multiple_of(b * blk, blk), blk), :], vst_sem.at[slot])

        x_copy(0, 0).start()
        load_k.start()
        load_v.start()
        load_q.start()
        z_copy(0).start()
        z_copy(1).start()

        @pl.when(middle)
        def _():
            z_copy(2).start()

        seg_at = lambda half, c: jnp.where(half == 0, c, n_seg - 1 - c) * seg

        def kv_region(half, c, which):
            at = pl.multiple_of(seg_at(half, c), seg)
            return kb.at[:, pl.ds(at // blk, seg // blk)] if which == 0 else vb.at[:, :, pl.ds(at, seg)]

        y_cp = (1 - cy) * 2 + cc
        c_cp = cy * 2 + 1 - cc
        yc_cp = (1 - cy) * 2 + 1 - cc

        def kv_send(half, which, kind):
            c, dev = ((cp, c_nb), (cp, y_nb), (y_cp, c_nb))[kind]
            region = kv_region(half, c, which)
            i = half * 2 + which
            return remote(region, region, kv_s.at[kind, i], kv_r.at[kind, i], dev)

        def kv_relay(half):
            for which in range(2):
                got(kv_region(half, y_cp, which), kv_r.at[1, half * 2 + which])
                kv_send(half, which, 2).start()

        def kv_arrived(half):
            for which in range(2):
                got(kv_region(half, c_cp, which), kv_r.at[0, half * 2 + which])
                got(kv_region(half, yc_cp, which), kv_r.at[2, half * 2 + which])

        def k_copy(half, hh):
            at = pl.multiple_of(seg_at(half, cp), seg)
            n = seg // blk
            return pltpu.make_async_copy(kb.at[hh, pl.ds(at // blk, n)], k_ref.at[pl.ds(half * n, n), :, pl.ds(hh * d, d)], kout_sem.at[half, hh])

        load_k.wait()
        load_v.wait()

        def h_rows(b):
            h0 = big[1, pl.ds(pl.multiple_of(b * blk, blk), blk), :]
            h1 = big[1, pl.ds(pl.multiple_of(rows + b * blk, blk), blk), :]
            return jnp.concatenate([h0, h1], axis=1)

        def kv_block(b, carry):
            slot = b % 2
            x_copy(b, slot).wait()

            @pl.when(b + 1 < n_blk)
            def _():
                x_copy(b + 1, 1 - slot).start()

            def norm_rows(i, carry):
                at = pl.multiple_of(i * nr, nr)
                xf = xb[slot, pl.ds(at, nr), :].astype(F32)
                inv = lax.rsqrt(jnp.mean(xf * xf, axis=-1, keepdims=True) + NORM_EPS)
                for i in range(width // d):
                    lanes = slice(i * d, (i + 1) * d)
                    h = ((xf[:, lanes] * inv) * gain_ref[i:i + 1, :].astype(F32)).astype(BF16)
                    row = b * blk + (0 if i * d < half_w else rows)
                    lane = (i * d) % half_w
                    big[1, pl.ds(pl.multiple_of(row, blk) + at, nr), lane:lane + d] = h
                return carry

            lax.fori_loop(0, blk // nr, norm_rows, 0)
            h = h_rows(b)
            make_angles(b)
            kv = jnp.dot(h, big[0, :, qw:qw + 2 * kvh * d], preferred_element_type=F32).astype(BF16)
            cos, sin = cos_sin(b)
            at = pl.multiple_of(seg_at(b // 4, cp) + (b % 4) * blk, blk)

            @pl.when(b >= 2)
            def _():
                v_copy(b - 2, slot).wait()

            for hh in range(kvh):
                kb[hh, at // blk] = rotate(kv[:, hh * d:(hh + 1) * d], cos, sin)
                vb[hh, :, pl.ds(at, blk)] = kv[:, (kvh + hh) * d:(kvh + hh + 1) * d].T
            vst[slot] = kv[:, kvh * d:]
            v_copy(b, slot).start()
            for half in range(2):
                @pl.when(b == half * 4 + 3)
                def _():
                    for which in range(2):
                        kv_send(half, which, 1).start()
                        kv_send(half, which, 0).start()
                    for hh in range(kvh):
                        k_copy(half, hh).start()
            return carry

        lax.fori_loop(0, n_blk, kv_block, 0)
        v_copy(n_blk - 2, 0).wait()
        v_copy(n_blk - 1, 1).wait()
        load_q.wait()

        def q_half(half):
            def q_block(i, carry):
                b = half * 4 + i
                cos, sin = cos_sin(b)
                q = jnp.dot(h_rows(b), big[0, :, 0:qw], preferred_element_type=F32).astype(BF16)
                at = pl.multiple_of(b * blk, blk)
                for j in range(qw // d):
                    qb[j, pl.ds(at, blk), :] = rotate(q[:, j * d:(j + 1) * d], cos, sin)
                return carry

            lax.fori_loop(0, 4, q_block, 0)

        def o_region(zz, rb, hh):
            return oall_ref.at[pl.ds((zz * kvh + hh) * group, group), pl.ds(pl.multiple_of(rb * blk, blk), blk), :]

        def o_own(rb, hh):
            return qb.at[pl.ds(hh * group, group), pl.ds(pl.multiple_of(rb * blk, blk), blk), :]

        def o_local(rb, hh):
            return pltpu.make_async_copy(o_own(rb, hh), o_region(z, rb, hh), o_l.at[rb, hh])

        def o_send(kind, rb, hh):
            if kind == 0:
                return remote(o_own(rb, hh), o_region(z, rb, hh), o_s.at[0, rb, hh], o_r.at[0, rb, hh], {"tp": partner})
            return remote(o_own(rb, hh), o_region(z, rb, hh), o_s.at[1, rb, hh], o_r.at[slot_out, rb, hh], {"tp": other_mid})

        def o_fwd(kind, rb, hh):
            zz = other_mid if kind == 0 else other_end
            return remote(o_region(zz, rb, hh), o_region(zz, rb, hh), f_s.at[kind, rb, hh], o_r.at[1 + kind, rb, hh], {"tp": partner})

        scores = (s_a, s_b)
        accs = (acc_a, acc_b)

        def unit(u):
            half, c, hh = u // 4, (u // 2) % 2, u % 2
            r0 = pl.multiple_of(half * seg + c * unit_rows, unit_rows)
            g0 = seg_at(half, cp) + c * unit_rows
            for st in range(2):
                for j in range(group):
                    blk_q = qb[hh * group + j, pl.ds(r0 + st * bq, bq), :]
                    qs = blk_q.T.astype(F32) * SCALE2
                    top = qs.astype(BF16)
                    span = slice(j * bq, (j + 1) * bq)
                    qt[st, 0:d, span] = top
                    qt[st, d:2 * d, span] = (qs - top.astype(F32)).astype(BF16)
            k_idx = lax.broadcasted_iota(jnp.int32, (bk, cols), 0)
            q_idx = lax.broadcasted_iota(jnp.int32, (bk, cols), 1) % bq

            def qk(st, t, mask=None):
                kt = kb[hh, pl.ds(t * (bk // blk), bk // blk)].reshape(bk, d)
                s = jnp.dot(jnp.concatenate([kt, kt], axis=1), qt[st], preferred_element_type=F32)
                if mask is not None:
                    s = jnp.where(mask, s, NEG)
                scores[st][...] = s
                m_tile[st] = jnp.max(s, axis=0, keepdims=True)

            def soft(st, t):
                m_old = m_run[st]
                m_new = jnp.maximum(m_old, m_tile[st])
                m_run[st] = m_new
                alpha = jnp.exp2(m_old - m_new)
                p = jnp.exp2(scores[st][...] - m_new)
                l_run[st] = l_run[st] * alpha + jnp.sum(p, axis=0, keepdims=True)
                pv = jnp.dot(vb[hh, :, pl.ds(pl.multiple_of(t * bk, bk), bk)], p.astype(BF16), preferred_element_type=F32)
                accs[st][...] = accs[st][...] * alpha + pv

            m_run[...] = jnp.full_like(m_run, NEG)
            l_run[...] = jnp.zeros_like(l_run)
            acc_a[...] = jnp.zeros_like(acc_a)
            acc_b[...] = jnp.zeros_like(acc_b)
            n_full = g0 // bk

            @pl.when(n_full > 0)
            def _():
                qk(0, 0)

            @pl.when(n_full == 0)
            def _():
                qk(0, 0, k_idx <= q_idx)

            def body(t, carry):
                qk(1, t)
                soft(0, t)
                qk(0, t + 1)
                soft(1, t)
                return carry

            lax.fori_loop(0, n_full - 1, body, 0)

            @pl.when(n_full > 0)
            def _():
                qk(1, n_full - 1)
                soft(0, n_full - 1)
                qk(0, n_full, k_idx <= q_idx)
                soft(1, n_full - 1)

            qk(1, n_full, k_idx <= q_idx + bq)
            soft(0, n_full)
            soft(1, n_full)
            for st in range(2):
                o = accs[st][...] * (1.0 / l_run[st])
                for j in range(group):
                    qb[hh * group + j, pl.ds(r0 + st * bq, bq), :] = o[:, j * bq:(j + 1) * bq].T.astype(BF16)
            for st in range(2):
                rb = half * 4 + c * 2 + st
                o_send(0, rb, hh).start()
                o_send(1, rb, hh).start()
                o_local(rb, hh).start()

        q_half(0)
        kv_relay(0)
        kv_arrived(0)


        def o_forward(rb):
            @pl.when(middle)
            def _():
                for kind, zz in ((0, other_mid), (1, other_end)):
                    for hh in range(kvh):
                        got(o_region(zz, rb, hh), o_r.at[1 + kind, rb, hh])
                        o_fwd(kind, rb, hh).start()

        def unit_loop(u, carry):
            @pl.when(u == 4)
            def _():
                @pl.when(middle)
                def _():
                    got(w_piece(other_end, 0, 0, 0), wz_r.at[2])
                    z_forward().start()

                kv_relay(1)
                q_half(1)
                for c in w_load_own():
                    c.start()
                kv_arrived(1)
                w_stage1(0)
                w_stage1(1)

            unit(u)

            @pl.when((u == 4) & middle)
            def _():
                w_stage1(2)

            @pl.when(u == 5)
            def _():
                o_forward(0)

            @pl.when(u == 6)
            def _():
                w_stage2(0)
                w_stage2(1)
                o_forward(1)
            return carry

        lax.fori_loop(0, 8, unit_loop, 0)

        def o_landed(kind, rb):
            for hh in range(kvh):
                if kind == 0:
                    o_local(rb, hh).wait()
                elif kind == 1:
                    got(o_region(partner, rb, hh), o_r.at[0, rb, hh])
                else:
                    @pl.when(jnp.logical_not(middle))
                    def _():
                        got(o_region(sources[kind], rb, hh), o_r.at[kind - 1, rb, hh])

        heads = kvh * group

        def ob_copy(kind, rb, slot):
            zz = sources[kind]
            return pltpu.make_async_copy(
                oall_ref.at[pl.ds(zz * heads, heads), pl.ds(pl.multiple_of(rb * blk, blk), blk), :],
                kb.at[slot, pl.ds(zz * heads, heads)], ob_sem.at[slot, kind])

        def o_fetch(rb, slot, kinds):
            for kind in kinds:
                o_landed(kind, rb)
                ob_copy(kind, rb, slot).start()

        n_y = width // y_cols
        n_h = half_w // y_cols

        def y_copy(rb, n, slot):
            return pltpu.make_async_copy(
                yb.at[slot],
                y_ref.at[pl.ds(pl.multiple_of(rb * blk, blk), blk), pl.ds(pl.multiple_of(n * y_cols, y_cols), y_cols)], yb_sem.at[slot])

        x_copy(0, 0).start()

        @pl.when(jnp.logical_not(middle))
        def _():
            w_stage1(2)

        o_forward(2)
        w_stage3(0)
        w_stage3(1)
        w_stage4(0)
        w_stage2(2)
        o_forward(3)
        w_stage4(1)
        w_stage3(2)
        w_stage4(2)
        for half in range(2):
            for which in range(2):
                for kind in range(3):
                    kv_send(half, which, kind).wait_send()
            for hh in range(kvh):
                k_copy(half, hh).wait()
        o_fetch(0, 0, range(4))
        for c in w_load_own() + w_load_other(0) + w_load_other(1) + w_load_other(2):
            c.wait()

        def product(slot, kinds, n):
            acc = None
            lane = pl.multiple_of((n % n_h) * y_cols, y_cols)
            for kind in kinds:
                zz = sources[kind]
                o = jnp.concatenate([kb[slot, zz * heads + i] for i in range(heads)], axis=1)
                w = big[n // n_h, pl.ds(pl.multiple_of(zz * qw, qw), qw), pl.ds(lane, y_cols)]
                term = jnp.dot(o, w, preferred_element_type=F32)
                acc = term if acc is None else acc + term
            return acc

        def x_cols(slot, n):
            return xb[slot, :, pl.ds(pl.multiple_of(n * y_cols, y_cols), y_cols)].astype(F32)

        def out_block(rb, carry):
            slot = rb % 2
            x_copy(rb, slot).wait()
            for kind in range(4):
                ob_copy(kind, rb, slot).wait()
            x_copy(rb + 1, 1 - slot).start()

            def out_cols(n, carry):
                ys = n % 2

                @pl.when(rb * n_y + n >= 2)
                def _():
                    y_copy(rb, n, ys).wait()

                yb[ys] = (x_cols(slot, n) + product(slot, range(4), n)).astype(BF16)
                y_copy(rb, n, ys).start()
                return carry

            lax.fori_loop(0, n_y, out_cols, 0)

            @pl.when(rb + 4 < n_blk)
            def _():
                o_forward(rb + 4)

            @pl.when(rb + 2 < n_blk)
            def _():
                o_fetch(rb + 1, 1 - slot, range(4))
            return carry

        lax.fori_loop(0, n_blk - 1, out_block, 0)

        last, slot = n_blk - 1, (n_blk - 1) % 2
        o_fetch(last, slot, range(3))
        x_copy(last, slot).wait()
        for kind in range(3):
            ob_copy(kind, last, slot).wait()

        def part(n):
            return (pl.ds(pl.multiple_of((n % n_h) // 2 * blk, blk), blk), pl.ds(pl.multiple_of(n % 2 * y_cols, y_cols), y_cols))

        for i in range(2):
            def first_terms(n, carry):
                scores[i][part(n)] = x_cols(slot, n) + product(slot, range(3), n)
                return carry

            lax.fori_loop(i * n_h, (i + 1) * n_h, first_terms, 0)
        o_fetch(last, slot, (3,))
        ob_copy(3, last, slot).wait()
        for i in range(2):
            def last_terms(n, carry):
                ys = n % 2
                y_copy(last, n, ys).wait()
                yb[ys] = (scores[i][part(n)] + product(slot, (3,), n)).astype(BF16)
                y_copy(last, n, ys).start()
                return carry

            lax.fori_loop(i * n_h, (i + 1) * n_h, last_terms, 0)
        for n in (n_y - 2, n_y - 1):
            y_copy(n_blk - 1, n, n % 2).wait()

        def drain(i, carry):
            rb, hh = i // kvh, i % kvh
            o_send(0, rb, hh).wait_send()
            o_send(1, rb, hh).wait_send()

            @pl.when(middle)
            def _():
                o_fwd(0, rb, hh).wait_send()
                o_fwd(1, rb, hh).wait_send()
            return carry

        lax.fori_loop(0, n_blk * kvh, drain, 0)
        z_copy(0).wait_send()
        z_copy(1).wait_send()

        @pl.when(middle)
        def _():
            z_copy(2).wait_send()
            z_forward().wait_send()

        for o in range(3):
            for kind in range(4):
                w_send(kind, o).wait_send()
                c_send(kind, o).wait_send()

    any_spec = pl.BlockSpec(memory_space=pl.ANY)
    vmem_spec = pl.BlockSpec(memory_space=pltpu.VMEM)
    dma = pltpu.SemaphoreType.DMA
    outs = pl.pallas_call(
        kernel,
        in_specs=[any_spec, vmem_spec] + [any_spec] * 4 + [pl.BlockSpec(memory_space=pltpu.SMEM), vmem_spec],
        out_specs=[any_spec] * 5,
        out_shape=[
            jax.ShapeDtypeStruct((rows, width), BF16),
            jax.ShapeDtypeStruct((n_blk, blk, kvh * d), BF16),
            jax.ShapeDtypeStruct((rows, kvh * d), BF16),
            jax.ShapeDtypeStruct((n_tp * kvh * group, rows, d), BF16),
            jax.ShapeDtypeStruct((width, width), BF16),
        ],
        scratch_shapes=[
            pltpu.VMEM((2, width, half_w), BF16),
            pltpu.VMEM((kvh, total // blk, blk, d), BF16),
            pltpu.VMEM((kvh, d, total), BF16),
            pltpu.VMEM((qw // d, rows, d), BF16),
            pltpu.VMEM((2, blk, width), BF16),
            pltpu.VMEM((rows, d), F32),
            pltpu.VMEM((2, blk, kvh * d), BF16),
            pltpu.VMEM((2, 2 * d, cols), BF16),
            pltpu.VMEM((bk, cols), F32),
            pltpu.VMEM((bk, cols), F32),
            pltpu.VMEM((d, cols), F32),
            pltpu.VMEM((d, cols), F32),
            pltpu.VMEM((2, 1, cols), F32),
            pltpu.VMEM((2, 1, cols), F32),
            pltpu.VMEM((2, 1, cols), F32),
            pltpu.VMEM((2, blk, y_cols), BF16),
            dma((3,)), dma((2,)), dma((2,)), dma((2, kvh)),
            dma((3, 4)), dma((3, 4)), dma((4,)), dma((3,)), dma((4, 3)), dma((4, 3)), dma((4, 3)), dma((4, 3)),
            dma((2, n_blk, kvh)), dma((n_blk, kvh)), dma((3, n_blk, kvh)), dma((2, n_blk, kvh)), dma((2, 4)), dma((2,)), dma((4, 2)),
        ],
        compiler_params=pltpu.CompilerParams(collective_id=0, has_side_effects=True, vmem_limit_bytes=67043328),
        name="sublayer",
    )(x, gain, w_q, w_k, w_v, w_o, positions, freqs)
    return outs[0], outs[1], outs[2]


def solution(mesh):
    def device_fn(x_in, positions, norm_gain, w_q, w_k, w_v, w_o):
        kv_heads = w_k.shape[1] // HEAD_DIM
        freqs = rope_freqs()
        freqs = jnp.concatenate([freqs, freqs])[None, :]
        gain = norm_gain.reshape(-1, HEAD_DIM)
        y, keys, values = layer(x_in, gain, w_q, w_k, w_v, w_o, positions, freqs)
        shape = (x_in.shape[0], kv_heads, HEAD_DIM)
        return y, keys.reshape(shape), values.reshape(shape)

    row_spec = P(('dp', 'cp'), None)
    cache_spec = P(('dp', 'cp'), 'tp', None)
    return jax.shard_map(device_fn, mesh=mesh, in_specs=(row_spec, P(('dp', 'cp')), P(None), P(None, 'tp'), P(None, 'tp'), P(None, 'tp'), P('tp', None)), out_specs=(row_spec, cache_spec, cache_spec), check_vma=False)
```

time: 2010 us -> 394 us (0.20)
  waiting for transfers between devices: 848 us -> 0 us
  other arithmetic: 616 us -> 0.61 us
  matrix products: 464 us -> 0 us
  Pallas kernels: 0 us -> 373 us
  local copies, waits for them, and re-layouts: 54.1 us -> 18.3 us
    sub x8 -> x0, other arithmetic: 574 us -> none  [one_block(): prob_bf = jax.nn.softmax(scores, axis=-1).astype(jnp.bfloat16)]
    reduce_scatter x1 -> x0, waiting for transfers between devices: 549 us -> none  [device_fn(): summed = lax.psum_scatter(part_out, 'tp', scatter_dimension=0, tiled=True)]
    dot_general x20 -> x0, matrix products: 464 us -> none  [the longest x8 212 us: one_block(): jnp.einsum('qhgd,thd->qhgt', q_part, keys, preferred_element_type=jnp.flo...]
    pallas_call x0 -> x1, Pallas kernels: none -> 373 us  [layer(): pl.pallas_call(kernel, in_specs=[any_spec, vmem_spec] + [any_spec] * 4 +...]
    all_gather x3 -> x0, waiting for transfers between devices: 299 us -> none  [the longest x1 285 us: device_fn(): y_out = lax.all_gather(y_share, 'tp', axis=0, tiled=True)]
    while x19 -> x0, local copies, waits for them, and re-layouts: 20.5 us -> none  [the longest x3 20.5 us: attend_all(): o_blocks = lax.map(one_block, (q_blocks, pos_blocks))]
  transfers between devices with their start and end apart: 4 -> 0, of which waited for: 3 -> 0; matrix products, arithmetic and copies ran while one was open for 3% -> 0% of each run, Pallas kernels for 0% -> 0%
where the time goes in v1:
time: 394 us; the launch traced here: 392 us
  Pallas kernels  373 us (95%)
  local copies, waits for them, and re-layouts  18.3 us (5%)
    pallas_call x1, Pallas kernels, layer(): pl.pallas_call(kernel, in_specs=[any_spec, vmem_spec] + [any_spec] * 4 +...  373 us
    unnamed x1, local copies, waits for them, and re-layouts  14.1 us

profile of v1, /device:TPU:0, one launch (start us, length us, event | category | flops | bytes accessed | tf_op | source)
XLA Modules:
  0.0 392.2 jit_solution(17121952403079879816)
XLA Ops:
  0.6 0.6 maximum_bitcast_fusion.freq_ref
  1.2 372.6 %sublayer.1 = (bf16[2048,4096]{1,0:T(8,128)(2,1)}, bf16[8,256,256]{2,1,0:T(8,128)(2,1)}, bf16[2048,256]{1,0:T(8,128)(2,1)}, bf16[32,2048,128]{2,1,0:T(8,128)(2,1)}, bf16[4096,4096]{1,0:T(8,128)(2,1)}) custom-call(bf16[2048,4096]{1,0:T(8,128)(2,1)} %x_ref.1, bf16[32,128]{1,0:T(8,128)(2,1)} %bitcast.3, bf16[4096,1024]{1,0:T(8,128)(2,1)} %wq_ref.1, ...), custom_call_target="tpu_custom_call" | custom-call | tf_op jit(solution)/shard_map/sublayer/pallas_call | solution.py:612
  373.8 2.1 reshape.16
  376.0 2.1 reshape.17
  378.1 14.1 %copy.11 = bf16[2048,4096]{1,0:T(8,128)(2,1)} copy(bf16[2048,4096]{1,0:T(8,128)(2,1)} %get-tuple-element.12) | data formatting | bytes 33554432
  (1 shorter events, 0.0 us)

commit v2 on v0

v2 whole, which is shorter than its diff:
```python
import math
import jax
import jax.numpy as jnp
from jax import lax
from jax.experimental import pallas as pl
from jax.experimental.pallas import tpu as pltpu
from jax.sharding import PartitionSpec as P

HEAD_DIM = 128
NORM_EPS = 1e-5
NEG = -0.7 * float(jnp.finfo(jnp.float32).max)
SCALE2 = (1.0 / math.sqrt(HEAD_DIM)) * math.log2(math.e)
BF16 = jnp.bfloat16
F32 = jnp.float32
MESH = pl.DeviceIdType.MESH
LOW, HIGH = range(2)
TOP, BOTTOM = range(2)
FIRST, SECOND, MOVED = SLOTS = range(3)
PARTNER, MID, END, SHIFTED = PIECES = range(4)


def rope_freqs():
    exponent = jnp.arange(0, HEAD_DIM, 2).astype(jnp.float32) / HEAD_DIM
    base_freq = 1.0 / (500000.0 ** exponent)
    wave_len = 2.0 * math.pi / base_freq
    smooth = (8192.0 / wave_len - 1.0) / 3.0
    blended = (1.0 - smooth) * base_freq / 8.0 + smooth * base_freq
    return jnp.where(wave_len < 2048.0, base_freq, jnp.where(wave_len > 8192.0, base_freq / 8.0, blended))


def repeat(n, step, first=0):
    lax.fori_loop(first, first + n, lambda i, carry: (step(i), carry)[1], 0)


def pick(i, values):
    out = values[-1]
    for at, value in enumerate(values[:-1]):
        out = jnp.where(i == at, value, out)
    return out


def rotate(vec_bf, cos, sin):
    vec = vec_bf.astype(F32)
    return (vec * cos + pltpu.roll(vec, HEAD_DIM // 2, axis=1) * sin).astype(BF16)


def layer(x, gain, w_q, w_k, w_v, w_o, positions, freqs):
    rows, width = x.shape
    seg = rows // 2
    d = HEAD_DIM
    kvh = w_k.shape[1] // d
    group = w_q.shape[1] // w_k.shape[1]
    gw = group * d
    qw = kvh * gw
    n_tp = width // qw
    n_groups = n_tp * kvh
    heads = n_groups * group
    n_seg = 8
    blk = 256
    n_blk = rows // blk
    n_lane = width // d
    half_w = width // 2
    bq, bk, bp = 256, 512, 256
    cols = bq * group
    unit_rows = 2 * bq
    w_slice = qw // 8
    s_slice = width // 8
    s_cols = gw + 2 * d
    s_at = qw
    y_cols = 512
    nr = 128
    assert n_blk == n_groups and heads == n_lane

    def kernel(x_ref, gain_ref, wq_ref, wk_ref, wv_ref, wo_ref, pos_ref, freq_ref,
               y_ref, k_ref, v_ref, oall_ref, wall_ref, wsx_ref,
               big, kb, vb, qb, csb, vst, qt, s_a, s_b, acc_a, acc_b, m_run, l_run, m_tile, yb,
               ld_sem, x_sem, vst_sem, kout_sem,
               kv_s, kv_r, wz_s, wz_r, sz_s, sz_r, wp_s, wp_r, wc_s, wc_r,
               o_s, o_l, o_r, f_s, ob_sem, yb_sem, wl_sem):
        dp, z, cp = lax.axis_index("dp"), lax.axis_index("tp"), lax.axis_index("cp")
        cy, cc = cp // 2, cp % 2
        x_nb = {"dp": 1 - dp}
        y_nb = {"cp": (1 - cy) * 2 + cc}
        c_nb = {"cp": cy * 2 + 1 - cc}

        middle = (z == 1) | (z == 2)
        end = jnp.logical_not(middle)
        partner = z + 1 - 2 * (z % 2)
        other_mid = jnp.where(z < 2, 2, 1)
        other_end = jnp.where(z < 2, 3, 0)
        sources = (z, partner, other_mid, other_end)
        slot_out = jnp.where(middle, MID, END)
        keep = jnp.where(z == 1, SECOND, FIRST)
        head_at = lambda slot: jnp.where(middle, keep, slot)
        last_z = n_tp - 1

        def group_of(zz, slot):
            at_far_end = n_groups - len(SLOTS) + (slot + 1) % len(SLOTS) if isinstance(slot, int) else (
                n_groups - len(SLOTS) + lax.rem(slot + 1, len(SLOTS)))
            return jnp.where(zz == 0, slot, jnp.where(zz == last_z, at_far_end, zz + kvh))

        source = lambda piece: sources[piece + 1]

        def remote(src, dst, ss, rs, dev):
            return pltpu.make_async_remote_copy(src_ref=src, dst_ref=dst, send_sem=ss, recv_sem=rs, device_id=dev, device_id_type=MESH)

        def got(region, rs):
            remote(region, region, rs, rs, x_nb).wait_recv()

        def at_rows(n, size):
            return pl.ds(pl.multiple_of(n, size), size)

        barrier = pltpu.get_barrier_semaphore()
        for dev in (x_nb, y_nb, c_nb, {"tp": partner}, {"tp": other_mid}, {"tp": other_end}):
            pl.semaphore_signal(barrier, inc=1, device_id=dev, device_id_type=MESH)
        pl.semaphore_wait(barrier, 6)

        place = dp * 4 + cp

        def place_of(fx, fy, fc):
            px = 1 - dp if fx else dp
            py = 1 - cy if fy else cy
            pc = 1 - cc if fc else cc
            return px * 4 + py * 2 + pc

        def piece(o, fx, fy, fc, part=None):
            size = s_slice if o == SHIFTED else w_slice
            base = place_of(fx, fy, fc) * size
            if o != SHIFTED:
                base = base + source(o) * qw
            n = size if part is None else size // 2
            base = pl.multiple_of(base + (n if part == BOTTOM else 0), n)
            return (wsx_ref if o == SHIFTED else wall_ref).at[pl.ds(base, n), :]

        here = lambda o: piece(o, 0, 0, 0)
        next_x = lambda o, part=None: piece(o, 1, 0, 0, part)
        next_y = lambda o, part=None: piece(o, 0, 1, 0, part)
        next_xy = lambda o, part=None: piece(o, 1, 1, 0, part)
        at_core = lambda o: (here(o), next_x(o), next_y(o), next_xy(o))

        def z_copy(o):
            src = wo_ref.at[at_rows(place * w_slice, w_slice), :]
            dst = wall_ref.at[at_rows(z * qw + place * w_slice, w_slice), :]
            return remote(src, dst, wz_s.at[o], wz_r.at[PARTNER if o == PARTNER else slot_out], {"tp": source(o)})

        def z_forward():
            return remote(here(END), here(END), wz_s.at[SHIFTED], wz_r.at[END], {"tp": partner})

        s_parts = ((wq_ref, 0, gw), (wk_ref, gw, d), (wv_ref, gw + d, d))

        def s_dst(i):
            _, lane, n = s_parts[i]
            return wsx_ref.at[at_rows(place * s_slice, s_slice), pl.ds(lane, n)]

        def s_copy(i):
            ref, _, n = s_parts[i]
            src = ref.at[at_rows(place * s_slice, s_slice), at_rows((1 - keep) * n, n)]
            return remote(src, s_dst(i), sz_s.at[i], sz_r.at[i], {"tp": partner})

        OWN_X, OWN_Y, X_TO_Y, Y_TO_X = kinds = range(4)

        def w_send(kind, o):
            if kind == OWN_X:
                region, dev = here(o), x_nb
            elif kind == OWN_Y:
                region, dev = here(o), y_nb
            elif kind == X_TO_Y:
                region, dev = next_x(o, TOP), y_nb
            else:
                region, dev = next_y(o, None if o == SHIFTED else BOTTOM), x_nb
            return remote(region, region, wp_s.at[kind, o], wp_r.at[kind, o], dev)

        def c_send(i, o):
            region = at_core(o)[i]
            return remote(region, region, wc_s.at[i, o], wc_r.at[i, o], c_nb)

        def w_stage1(o):
            if o == SHIFTED:
                for i in range(len(s_parts)):
                    got(s_dst(i), sz_r.at[i])
            elif o != END:
                got(here(o), wz_r.at[o])
            else:
                @pl.when(end)
                def _():
                    got(here(o), wz_r.at[o])

            w_send(OWN_X, o).start()
            w_send(OWN_Y, o).start()
            c_send(0, o).start()

        def w_stage2(o):
            got(next_x(o), wp_r.at[OWN_X, o])
            if o != SHIFTED:
                w_send(X_TO_Y, o).start()
            c_send(1, o).start()
            got(next_y(o), wp_r.at[OWN_Y, o])
            w_send(Y_TO_X, o).start()
            c_send(2, o).start()

        def w_stage3(o):
            if o != SHIFTED:
                got(next_xy(o, TOP), wp_r.at[X_TO_Y, o])
            got(next_xy(o, None if o == SHIFTED else BOTTOM), wp_r.at[Y_TO_X, o])
            c_send(3, o).start()

        def w_gathered(o):
            for i, (fx, fy) in enumerate(((0, 0), (1, 0), (0, 1), (1, 1))):
                got(piece(o, fx, fy, 1), wc_r.at[i, o])

        def w_load(zs, src, i):
            return [pltpu.make_async_copy(
                src.at[:, pl.ds(n * half_w, half_w)], big.at[n, at_rows(zs * qw, qw), :], wl_sem.at[i, n]) for n in range(2)]

        def w_load_own():
            return w_load(z, wo_ref, SHIFTED)

        def w_load_other(o):
            return w_load(source(o), wall_ref.at[at_rows(source(o) * qw, qw), :], o)

        def w_stage4(o):
            w_gathered(o)
            for c in w_load_other(o):
                c.start()

        def load_weights(i, ref, lane, n):
            return pltpu.make_async_copy(ref, big.at[0, :, pl.ds(lane, n)], ld_sem.at[i])

        load_q, load_k, load_v, load_s = (load_weights(i, *args) for i, args in enumerate((
            (wq_ref, 0, qw), (wk_ref, qw, kvh * d), (wv_ref, qw + kvh * d, kvh * d), (wsx_ref, s_at, s_cols))))

        def x_start(b, slot):
            for i in range(n_lane):
                pltpu.make_async_copy(x_ref.at[at_rows(b * blk, blk), pl.ds(i * d, d)], kb.at[2 + slot, i], x_sem.at[slot]).start()

        def x_wait(slot):
            pltpu.make_async_copy(kb.at[2 + slot], kb.at[2 + slot], x_sem.at[slot]).wait()

        def v_copy(b):
            return pltpu.make_async_copy(vst, v_ref.at[at_rows(b * blk, blk), :], vst_sem.at[0])

        low_lanes = lax.broadcasted_iota(jnp.int32, (blk, d), 1) < d // 2

        def make_angles(b):
            first = pos_ref[b * blk]
            pos = (lax.broadcasted_iota(jnp.int32, (blk, d), 0) + first).astype(F32)
            angle = pos * freq_ref[...]
            csb[at_rows(b * blk, blk), :] = jnp.where(low_lanes, jnp.cos(angle), jnp.sin(angle))

        def cos_sin(b):
            both = csb[at_rows(b * blk, blk), :]
            turned = pltpu.roll(both, d // 2, axis=1)
            return jnp.where(low_lanes, both, turned), jnp.where(low_lanes, -turned, both)

        x_start(0, 0)
        load_k.start()
        load_v.start()
        load_q.start()

        @pl.when(middle)
        def _():
            for i in range(len(s_parts)):
                s_copy(i).start()

        z_copy(PARTNER).start()
        z_copy(MID).start()

        @pl.when(middle)
        def _():
            z_copy(END).start()

        seg_at = lambda half, c: jnp.where(half == LOW, c, n_seg - 1 - c) * seg
        y_cp = (1 - cy) * 2 + cc
        c_cp = cy * 2 + 1 - cc
        yc_cp = (1 - cy) * 2 + 1 - cc

        def kv_region(half, c, which, slot):
            at = pl.multiple_of(seg_at(half, c), seg)
            h = head_at(slot)
            return kb.at[h, pl.ds(at // blk, seg // blk)] if which == 0 else vb.at[h, :, pl.ds(at, seg)]

        TO_CORE, TO_Y, Y_TO_CORE = kv_kinds = range(3)
        kv_both = range(2)
        n_kv = len(kv_both) * len(SLOTS)
        kv_at = lambda half, which, slot: half * n_kv + which * len(SLOTS) + slot

        def kv_send(kind, half, which, slot):
            region = kv_region(half, y_cp if kind == Y_TO_CORE else cp, which, slot)
            i = kv_at(half, which, slot)
            return remote(region, region, kv_s.at[kind, i], kv_r.at[kind, i], y_nb if kind == TO_Y else c_nb)

        def for_slots(slots, f):
            for slot in slots:
                if slot == FIRST:
                    f(slot)
                else:
                    @pl.when(end)
                    def _():
                        f(slot)

        own = (FIRST, SECOND)
        moved = (MOVED,)

        def kv_start(half, slots):
            def f(slot):
                for which in kv_both:
                    kv_send(TO_Y, half, which, slot).start()
                    kv_send(TO_CORE, half, which, slot).start()
            for_slots(slots, f)

        def kv_relay(half, slots):
            def f(slot):
                for which in kv_both:
                    got(kv_region(half, y_cp, which, slot), kv_r.at[TO_Y, kv_at(half, which, slot)])
                    kv_send(Y_TO_CORE, half, which, slot).start()
            for_slots(slots, f)

        def kv_arrived(half, slots):
            def f(slot):
                for which in kv_both:
                    i = kv_at(half, which, slot)
                    got(kv_region(half, c_cp, which, slot), kv_r.at[TO_CORE, i])
                    got(kv_region(half, yc_cp, which, slot), kv_r.at[Y_TO_CORE, i])
            for_slots(slots, f)

        def kv_sent():
            def f(slot):
                for half in (LOW, HIGH):
                    for which in kv_both:
                        for kind in kv_kinds:
                            kv_send(kind, half, which, slot).wait_send()
            for_slots(SLOTS, f)

        def k_copy(half, hh):
            at = pl.multiple_of(seg_at(half, cp), seg)
            n = seg // blk
            return pltpu.make_async_copy(kb.at[hh, pl.ds(at // blk, n)], k_ref.at[pl.ds(half * n, n), :, pl.ds(hh * d, d)], kout_sem.at[half, hh])

        def h_rows(b):
            h0 = big[1, at_rows(b * blk, blk), :]
            h1 = big[1, at_rows(rows + b * blk, blk), :]
            return jnp.concatenate([h0, h1], axis=1)

        load_k.wait()
        load_v.wait()

        half_blk = n_blk // 2

        def at_half_end(b, f):
            for half in (LOW, HIGH):
                @pl.when(b == half * half_blk + half_blk - 1)
                def _():
                    f(half)

        def kv_rows(b):
            return pl.multiple_of(seg_at(b // half_blk, cp) + lax.rem(b, half_blk) * blk, blk)

        def kv_block(b):
            slot = b % 2
            x_wait(slot)

            @pl.when(b + 1 < n_blk)
            def _():
                x_start(b + 1, 1 - slot)

            def norm_rows(i):
                at = at_rows(i * nr, nr)
                square = 0.0
                for j in range(n_lane):
                    xf = kb[2 + slot, j, at, :].astype(F32)
                    square = square + xf * xf
                inv = lax.rsqrt(jnp.sum(square, axis=-1, keepdims=True) / width + NORM_EPS)
                for j in range(n_lane):
                    xf = kb[2 + slot, j, at, :].astype(F32)
                    h = ((xf * inv) * gain_ref[j:j + 1, :].astype(F32)).astype(BF16)
                    row = b * blk + (0 if j * d < half_w else rows) + i * nr
                    lane = (j * d) % half_w
                    big[1, at_rows(row, nr), lane:lane + d] = h

            repeat(blk // nr, norm_rows)
            make_angles(b)
            kv = jnp.dot(h_rows(b), big[0, :, qw:qw + 2 * kvh * d], preferred_element_type=F32).astype(BF16)
            cos, sin = cos_sin(b)
            at = kv_rows(b)

            @pl.when(b > 0)
            def _():
                v_copy(b - 1).wait()

            for hh in range(kvh):
                kb[hh, at // blk] = rotate(kv[:, hh * d:(hh + 1) * d], cos, sin)
                vb[hh, :, pl.ds(at, blk)] = kv[:, (kvh + hh) * d:(kvh + hh + 1) * d].T
            vst[...] = kv[:, kvh * d:]
            v_copy(b).start()

            def send(half):
                kv_start(half, own)
                for hh in range(kvh):
                    k_copy(half, hh).start()

            at_half_end(b, send)

        repeat(n_blk, kv_block)
        v_copy(n_blk - 1).wait()
        load_q.wait()

        @pl.when(end)
        def _():
            w_stage1(SHIFTED)

        def q_half(half):
            def q_block(b):
                cos, sin = cos_sin(b)

                def project(i):
                    head = head_at(i)
                    q = jnp.dot(h_rows(b), big[0, :, at_rows(head * gw, gw)], preferred_element_type=F32).astype(BF16)
                    for j in range(group):
                        qb[head * group + j, at_rows(b * blk, blk), :] = rotate(q[:, j * d:(j + 1) * d], cos, sin)

                repeat(jnp.where(middle, 1, kvh), project)

            repeat(half_blk, q_block, half * half_blk)

        def moved_block(b):
            cos, sin = cos_sin(b)
            qkv = jnp.dot(h_rows(b), big[0, :, s_at:s_at + s_cols], preferred_element_type=F32).astype(BF16)
            for j in range(group):
                qb[MOVED * group + j, at_rows(b * blk, blk), :] = rotate(qkv[:, j * d:(j + 1) * d], cos, sin)
            at = kv_rows(b)
            kb[MOVED, at // blk] = rotate(qkv[:, gw:gw + d], cos, sin)
            vb[MOVED, :, pl.ds(at, blk)] = qkv[:, gw + d:].T
            at_half_end(b, lambda half: kv_start(half, moved))

        def o_region(g, rb):
            return oall_ref.at[pl.ds(g * group, group), at_rows(rb * blk, blk), :]

        def o_own(slot, rb):
            return qb.at[pl.ds(head_at(slot) * group, group), at_rows(rb * blk, blk), :]

        def o_local(slot, rb):
            return pltpu.make_async_copy(o_own(slot, rb), o_region(group_of(z, slot), rb), o_l.at[rb, slot])

        def o_send(to, slot, rb):
            g = group_of(z, slot)
            return remote(o_own(slot, rb), o_region(g, rb), o_s.at[to, rb, slot], o_r.at[rb, g], {"tp": source(to)})

        others = ((MID, FIRST), (END, FIRST), (END, SECOND), (END, MOVED))
        ends_own = ((PARTNER, FIRST), (PARTNER, SECOND), (PARTNER, MOVED))
        passed = others + ends_own

        def o_pass(what, rb):
            g = group_of(source(what[0]), what[1])
            region = o_region(g, rb)
            to = {"tp": partner if what in others else other_mid}
            return remote(region, region, f_s.at[rb, passed.index(what)], o_r.at[rb, g], to)

        def o_wait(what, rb):
            g = group_of(source(what[0]), what[1])
            got(o_region(g, rb), o_r.at[rb, g])

        def pass_on(what, blocks):
            def step(rb):
                for item in what:
                    o_wait(item, rb)
                    o_pass(item, rb).start()

            repeat(len(blocks), step, blocks[0])

        def own_outward(blocks):
            repeat(len(blocks), lambda rb: o_send(PARTNER, FIRST, rb).start(), blocks[0])

        scores = (s_a, s_b)
        accs = (acc_a, acc_b)

        def unit(half, c, slot):
            hl = head_at(slot)
            r0 = pl.multiple_of(half * seg + c * unit_rows, unit_rows)
            g0 = seg_at(half, cp) + c * unit_rows
            for st in range(2):
                for j in range(group):
                    qs = qb[hl * group + j, pl.ds(r0 + st * bq, bq), :].T.astype(F32) * SCALE2
                    top = qs.astype(BF16)
                    span = slice(j * bq, (j + 1) * bq)
                    qt[st, 0:d, span] = top
                    qt[st, d:2 * d, span] = (qs - top.astype(F32)).astype(BF16)
            k_idx = lax.broadcasted_iota(jnp.int32, (bk, cols), 0)
            q_idx = lax.broadcasted_iota(jnp.int32, (bk, cols), 1) % bq

            def qk(st, t, mask=None):
                kt = kb[hl, pl.ds(t * (bk // blk), bk // blk)].reshape(bk, d)
                s = jnp.dot(jnp.concatenate([kt, kt], axis=1), qt[st], preferred_element_type=F32)
                if mask is not None:
                    s = jnp.where(mask, s, NEG)
                scores[st][...] = s
                m_tile[st] = jnp.max(s, axis=0, keepdims=True)

            def soft(st, t):
                m_old = m_run[st]
                m_new = jnp.maximum(m_old, m_tile[st])
                m_run[st] = m_new
                alpha = jnp.exp2(m_old - m_new)
                total, pv = 0.0, 0.0
                for i in range(bk // bp):
                    p = jnp.exp2(scores[st][i * bp:(i + 1) * bp, :] - m_new)
                    total = total + jnp.sum(p, axis=0, keepdims=True)
                    v = vb[hl, :, at_rows(t * bk + i * bp, bp)]
                    pv = pv + jnp.dot(v, p.astype(BF16), preferred_element_type=F32)
                l_run[st] = l_run[st] * alpha + total
                accs[st][...] = accs[st][...] * alpha + pv

            m_run[...] = jnp.full_like(m_run, NEG)
            l_run[...] = jnp.zeros_like(l_run)
            acc_a[...] = jnp.zeros_like(acc_a)
            acc_b[...] = jnp.zeros_like(acc_b)
            n_full = g0 // bk

            @pl.when(n_full > 0)
            def _():
                qk(0, 0)

            @pl.when(n_full == 0)
            def _():
                qk(0, 0, k_idx <= q_idx)

            def body(t):
                qk(1, t)
                soft(0, t)
                qk(0, t + 1)
                soft(1, t)

            repeat(n_full - 1, body)

            @pl.when(n_full > 0)
            def _():
                qk(1, n_full - 1)
                soft(0, n_full - 1)
                qk(0, n_full, k_idx <= q_idx)
                soft(1, n_full - 1)

            qk(1, n_full, k_idx <= q_idx + bq)
            soft(0, n_full)
            soft(1, n_full)
            for st in range(2):
                o = accs[st][...] * (1.0 / l_run[st])
                for j in range(group):
                    qb[hl * group + j, pl.ds(r0 + st * bq, bq), :] = o[:, j * bq:(j + 1) * bq].T.astype(BF16)
            for st in range(2):
                rb = half * half_blk + c * 2 + st

                @pl.when(middle)
                def _():
                    o_send(MID, slot, rb).start()

                @pl.when(end | (half == LOW))
                def _():
                    o_send(PARTNER, slot, rb).start()

                o_local(slot, rb).start()

        q_half(LOW)
        kv_relay(LOW, own)
        kv_arrived(LOW, own)

        def when_cp(which, f):
            @pl.when(which)
            def _():
                f()

        def nothing():
            pass

        def start_all(copies):
            for c in copies:
                c.start()

        def second_half():
            when_cp(cp > 0, lambda: kv_relay(HIGH, own))
            when_cp(cp == 3, lambda: w_stage2(SHIFTED))
            q_half(HIGH)
            when_cp(cp == 0, lambda: kv_relay(HIGH, own))
            kv_arrived(HIGH, own)
            when_cp(cp == 2, lambda: w_stage2(SHIFTED))
            when_cp(cp >= 2, lambda: w_stage1(PARTNER))

        def moved_head():
            w_gathered(SHIFTED)
            load_s.start()
            load_s.wait()
            repeat(n_blk, moved_block)
            start_all(w_load_own())
            when_cp(cp >= 2, lambda: w_stage2(PARTNER))
            w_stage1(END)

        def after_e():
            when_cp(cp < 2, lambda: w_stage2(SHIFTED))
            when_cp(cp == 3, lambda: w_stage3(SHIFTED))
            w_stage1(MID)

        def after_f():
            when_cp(cp < 3, lambda: w_stage3(SHIFTED))
            when_cp(cp < 2, lambda: w_stage2(PARTNER))

        def after_g():
            kv_relay(LOW, moved)
            w_stage2(MID)
            kv_arrived(LOW, moved)

        def after_h():
            kv_relay(HIGH, moved)

        def after_i():
            kv_arrived(HIGH, moved)

        def after_j():
            w_stage3(PARTNER)
            w_stage2(END)

        def after_k():
            w_stage3(MID)
            w_stage4(PARTNER)

        def after_l():
            w_stage3(END)
            w_stage4(MID)
            w_stage4(END)

        end_units = (
            (LOW, TOP, FIRST, nothing, nothing),
            (LOW, TOP, SECOND, nothing, nothing),
            (LOW, BOTTOM, FIRST, nothing, nothing),
            (LOW, BOTTOM, SECOND, nothing, lambda: when_cp(cp < 2, lambda: w_stage1(PARTNER))),
            (HIGH, TOP, FIRST, second_half, after_e),
            (HIGH, TOP, SECOND, nothing, after_f),
            (HIGH, BOTTOM, FIRST, moved_head, after_g),
            (LOW, TOP, MOVED, nothing, after_h),
            (LOW, BOTTOM, MOVED, nothing, after_i),
            (HIGH, TOP, MOVED, nothing, after_j),
            (HIGH, BOTTOM, SECOND, nothing, after_k),
            (HIGH, BOTTOM, MOVED, nothing, after_l),
        )

        low_blocks, high_blocks = range(half_blk), range(half_blk, n_blk)
        top = lambda blocks: blocks[:half_blk // 2]
        bottom = lambda blocks: blocks[half_blk // 2:]
        mids, end_first, end_both, end_moved = others[:1], others[1:2], others[1:3], others[3:]
        own_both, own_moved = ends_own[:2], ends_own[2:]

        def middle_high():
            got(here(END), wz_r.at[END])
            z_forward().start()
            kv_relay(HIGH, own)
            q_half(HIGH)
            kv_arrived(HIGH, own)
            start_all(w_load_own())
            for o in (PARTNER, MID, END):
                w_stage1(o)

        middle_units = (
            (LOW, TOP, FIRST, nothing, nothing),
            (LOW, BOTTOM, FIRST, nothing, nothing),
            (HIGH, TOP, FIRST, middle_high, lambda: pass_on(own_both, top(low_blocks))),
            (HIGH, BOTTOM, FIRST, nothing, nothing),
        )

        def unit_loop(s):
            half, c, slot = (
                jnp.where(middle, pick(s, [u[i] for u in middle_units]), pick(s, [u[i] for u in end_units])) for i in range(3))

            def events(i):
                for role, units in ((middle, middle_units), (end, end_units)):
                    for step, what in enumerate(units):
                        if what[i] is not nothing:
                            @pl.when(role & (s == step))
                            def _():
                                what[i]()

            events(-2)
            unit(half, c, slot)
            events(-1)

        repeat(jnp.where(middle, len(middle_units), len(end_units)), unit_loop)

        @pl.when(middle)
        def _():
            pass_on(own_both, bottom(low_blocks))
            pass_on(mids, low_blocks)
            w_stage2(PARTNER)
            pass_on(end_both, top(low_blocks))
            own_outward(top(high_blocks))
            w_stage2(MID)
            w_stage2(END)
            w_stage3(PARTNER)
            pass_on(end_both, bottom(low_blocks))
            w_stage3(MID)
            w_stage4(PARTNER)
            w_stage3(END)
            w_stage4(MID)
            pass_on(own_moved, low_blocks)
            w_stage4(END)
            pass_on(end_moved, low_blocks)
            pass_on(own_both, top(high_blocks))
            pass_on(mids, top(high_blocks))

        def middle_0():
            pass_on(own_moved, top(high_blocks))
            pass_on(end_both, top(high_blocks))

        def middle_1():
            pass_on(end_moved, top(high_blocks))
            own_outward(bottom(high_blocks))
            pass_on(mids, bottom(high_blocks))
            pass_on(own_both, bottom(high_blocks))

        def middle_2():
            pass_on(own_moved, bottom(high_blocks))
            pass_on(end_both, bottom(high_blocks))

        middle_events = (middle_0, middle_1, middle_2, lambda: pass_on(end_moved, bottom(high_blocks)))

        kv_sent()
        for half in range(2):
            for hh in range(kvh):
                k_copy(half, hh).wait()

        def early_landed(rb):
            for_slots(SLOTS, lambda slot: o_local(slot, rb).wait())

            @pl.when(end)
            def _():
                for what in (ends_own[0], others[0]):
                    o_wait(what, rb)

        def late_landed(rb):
            @pl.when(end)
            def _():
                for what in others[1:]:
                    o_wait(what, rb)

        def ob_copy(rb, slot, first, n, i):
            return pltpu.make_async_copy(
                oall_ref.at[pl.ds(first, n), at_rows(rb * blk, blk), :], kb.at[slot, pl.ds(first, n)], ob_sem.at[slot, i])

        def ob_all(rb, slot):
            return ob_copy(rb, slot, 0, heads, 0)

        def o_fetch(rb, slot):
            early_landed(rb)
            late_landed(rb)
            ob_all(rb, slot).start()

        n_y = width // y_cols
        n_h = half_w // y_cols

        def y_copy(rb, n, slot):
            return pltpu.make_async_copy(yb.at[slot], y_ref.at[at_rows(rb * blk, blk), at_rows(n * y_cols, y_cols)], yb_sem.at[slot])

        def product(slot, first, n_heads, n):
            o = jnp.concatenate([kb[slot, first + i] for i in range(n_heads)], axis=1)
            row = first * d if isinstance(first, int) else pl.multiple_of(first * d, gw)
            w = big[n // n_h, pl.ds(row, n_heads * d), at_rows((n % n_h) * y_cols, y_cols)]
            return jnp.dot(o, w, preferred_element_type=F32)

        def x_cols(slot, n):
            n_in = y_cols // d
            return jnp.concatenate([kb[2 + slot, n * n_in + i] for i in range(n_in)], axis=1).astype(F32)

        x_start(0, 0)
        o_fetch(0, 0)
        for c in sum((w_load_other(o) for o in (PARTNER, MID, END)), w_load_own()):
            c.wait()

        n_full_blocks = n_blk - 2

        def out_block(rb):
            slot = rb % 2
            x_wait(slot)
            ob_all(rb, slot).wait()
            x_start(rb + 1, 1 - slot)

            @pl.when(rb + 1 < n_full_blocks)
            def _():
                o_fetch(rb + 1, 1 - slot)

            def out_cols(n):
                ys = n % 2

                @pl.when(rb * n_y + n >= 2)
                def _():
                    y_copy(rb, n, ys).wait()

                yb[ys] = (x_cols(slot, n) + product(slot, 0, heads, n)).astype(BF16)
                y_copy(rb, n, ys).start()

            repeat(n_y, out_cols)
            for i, event in enumerate(middle_events):
                @pl.when(middle & (rb == i))
                def _():
                    event()

        repeat(n_full_blocks, out_block)

        n_late = len(SLOTS) * group
        n_early = heads - n_late
        early = jnp.where(z < 2, 0, n_late)
        late = jnp.where(z < 2, n_early, 0)
        blocks = (n_full_blocks, n_full_blocks + 1)

        def part(n):
            return (at_rows((n % n_h) // 2 * blk, blk), at_rows(n % 2 * y_cols, y_cols))

        def lanes_of(n, half):
            return at_rows(n * 2 * y_cols + half * y_cols, y_cols)

        def early_sum(slot, n):
            return x_cols(slot, n) + product(slot, early, n_early, n)

        def finish(slot, n, total):
            ys = n % 2
            y_copy(blocks[slot], n, ys).wait()
            yb[ys] = (total + product(slot, late, n_late, n)).astype(BF16)
            y_copy(blocks[slot], n, ys).start()

        early_copies = [ob_copy(rb, slot, early, n_early, 0) for slot, rb in enumerate(blocks)]
        late_copies = [ob_copy(rb, slot, late, n_late, 1) for slot, rb in enumerate(blocks)]
        for slot, rb in enumerate(blocks):
            early_landed(rb)
            if slot > 0:
                x_start(rb, slot)
            early_copies[slot].start()
        for i in range(2):
            if i == 0:
                x_wait(0)
                early_copies[0].wait()

            def first_terms(n):
                scores[i][part(n)] = early_sum(0, n)

            repeat(n_h, first_terms, i * n_h)
        x_wait(1)
        early_copies[1].wait()
        half_rows = blk // 2

        def second_terms(n):
            total = early_sum(1, n)
            for i in range(len(SLOTS)):
                term = total.astype(BF16)
                for half in range(2):
                    vb[i, :, lanes_of(n, half)] = term[half * half_rows:(half + 1) * half_rows]
                total = total - term.astype(F32)

        repeat(n_y, second_terms)
        late_landed(blocks[0])
        late_copies[0].start()
        late_copies[0].wait()
        for i in range(2):
            repeat(n_h, lambda n: finish(0, n, scores[i][part(n)]), i * n_h)
        late_landed(blocks[1])
        late_copies[1].start()
        late_copies[1].wait()

        def last_terms(n):
            terms = [jnp.concatenate([vb[i, :, lanes_of(n, half)] for half in range(2)], axis=0).astype(F32) for i in range(len(SLOTS))]
            finish(1, n, (terms[0] + terms[1]) + terms[2])

        repeat(n_y, last_terms)
        for n in (n_y - 2, n_y - 1):
            y_copy(blocks[1], n, n % 2).wait()

        def drain(rb):
            for_slots(SLOTS, lambda slot: o_send(PARTNER, slot, rb).wait_send())

            @pl.when(middle)
            def _():
                o_send(MID, FIRST, rb).wait_send()
                for what in passed:
                    o_pass(what, rb).wait_send()

        repeat(n_blk, drain)
        z_copy(PARTNER).wait_send()
        z_copy(MID).wait_send()

        @pl.when(middle)
        def _():
            z_copy(END).wait_send()
            z_forward().wait_send()
            for i in range(len(s_parts)):
                s_copy(i).wait_send()

        def w_sent(o):
            for kind in kinds:
                if (kind, o) != (X_TO_Y, SHIFTED):
                    w_send(kind, o).wait_send()
                c_send(kind, o).wait_send()

        for o in (PARTNER, MID, END):
            w_sent(o)

        @pl.when(end)
        def _():
            w_sent(SHIFTED)

    any_spec = pl.BlockSpec(memory_space=pl.ANY)
    vmem_spec = pl.BlockSpec(memory_space=pltpu.VMEM)
    dma = pltpu.SemaphoreType.DMA
    outs = pl.pallas_call(
        kernel,
        in_specs=[any_spec, vmem_spec] + [any_spec] * 4 + [pl.BlockSpec(memory_space=pltpu.SMEM), vmem_spec],
        out_specs=[any_spec] * 6,
        out_shape=[
            jax.ShapeDtypeStruct((rows, width), BF16),
            jax.ShapeDtypeStruct((n_blk, blk, kvh * d), BF16),
            jax.ShapeDtypeStruct((rows, kvh * d), BF16),
            jax.ShapeDtypeStruct((heads, rows, d), BF16),
            jax.ShapeDtypeStruct((width, width), BF16),
            jax.ShapeDtypeStruct((width, s_cols), BF16),
        ],
        scratch_shapes=[
            pltpu.VMEM((2, width, half_w), BF16),
            pltpu.VMEM((4, n_lane, blk, d), BF16),
            pltpu.VMEM((3, d, n_seg * seg), BF16),
            pltpu.VMEM((3 * group, rows, d), BF16),
            pltpu.VMEM((rows, d), F32),
            pltpu.VMEM((blk, kvh * d), BF16),
            pltpu.VMEM((2, 2 * d, cols), BF16),
            pltpu.VMEM((bk, cols), F32),
            pltpu.VMEM((bk, cols), F32),
            pltpu.VMEM((d, cols), F32),
            pltpu.VMEM((d, cols), F32),
            pltpu.VMEM((2, 1, cols), F32),
            pltpu.VMEM((2, 1, cols), F32),
            pltpu.VMEM((2, 1, cols), F32),
            pltpu.VMEM((2, blk, y_cols), BF16),
            dma((4,)), dma((2,)), dma((1,)), dma((2, kvh)),
            dma((3, 12)), dma((3, 12)), dma((4,)), dma((3,)), dma((3,)), dma((3,)), dma((4, 4)), dma((4, 4)), dma((4, 4)), dma((4, 4)),
            dma((2, n_blk, 3)), dma((n_blk, 3)), dma((n_blk, n_groups)), dma((n_blk, 7)), dma((2, 2)), dma((2,)), dma((4, 2)),
        ],
        compiler_params=pltpu.CompilerParams(collective_id=0, has_side_effects=True, vmem_limit_bytes=67043328),
        name="sublayer",
    )(x, gain, w_q, w_k, w_v, w_o, positions, freqs)
    return outs[0], outs[1], outs[2]


def solution(mesh):
    def device_fn(x_in, positions, norm_gain, w_q, w_k, w_v, w_o):
        kv_heads = w_k.shape[1] // HEAD_DIM
        freqs = rope_freqs()
        freqs = jnp.concatenate([freqs, freqs])[None, :]
        gain = norm_gain.reshape(-1, HEAD_DIM)
        y, keys, values = layer(x_in, gain, w_q, w_k, w_v, w_o, positions, freqs)
        shape = (x_in.shape[0], kv_heads, HEAD_DIM)
        return y, keys.reshape(shape), values.reshape(shape)

    row_spec = P(('dp', 'cp'), None)
    cache_spec = P(('dp', 'cp'), 'tp', None)
    return jax.shard_map(device_fn, mesh=mesh, in_specs=(row_spec, P(('dp', 'cp')), P(None), P(None, 'tp'), P(None, 'tp'), P(None, 'tp'), P('tp', None)), out_specs=(row_spec, cache_spec, cache_spec), check_vma=False)
```

time: 2010 us -> 357 us (0.18)
  waiting for transfers between devices: 848 us -> 0 us
  other arithmetic: 616 us -> 0.61 us
  matrix products: 464 us -> 0 us
  Pallas kernels: 0 us -> 337 us
  local copies, waits for them, and re-layouts: 54.1 us -> 18.3 us
    sub x8 -> x0, other arithmetic: 574 us -> none  [one_block(): prob_bf = jax.nn.softmax(scores, axis=-1).astype(jnp.bfloat16)]
    reduce_scatter x1 -> x0, waiting for transfers between devices: 549 us -> none  [device_fn(): summed = lax.psum_scatter(part_out, 'tp', scatter_dimension=0, tiled=True)]
    dot_general x20 -> x0, matrix products: 464 us -> none  [the longest x8 212 us: one_block(): jnp.einsum('qhgd,thd->qhgt', q_part, keys, preferred_element_type=jnp.flo...]
    pallas_call x0 -> x1, Pallas kernels: none -> 337 us  [layer(): pl.pallas_call(kernel, in_specs=[any_spec, vmem_spec] + [any_spec] * 4 +...]
    all_gather x3 -> x0, waiting for transfers between devices: 299 us -> none  [the longest x1 285 us: device_fn(): y_out = lax.all_gather(y_share, 'tp', axis=0, tiled=True)]
    while x19 -> x0, local copies, waits for them, and re-layouts: 20.5 us -> none  [the longest x3 20.5 us: attend_all(): o_blocks = lax.map(one_block, (q_blocks, pos_blocks))]
  transfers between devices with their start and end apart: 4 -> 0, of which waited for: 3 -> 0; matrix products, arithmetic and copies ran while one was open for 3% -> 0% of each run, Pallas kernels for 0% -> 0%
where the time goes in v2:
time: 357 us; the launch traced here: 356 us
  Pallas kernels  337 us (94%)
  local copies, waits for them, and re-layouts  18.3 us (5%)
    pallas_call x1, Pallas kernels, layer(): pl.pallas_call(kernel, in_specs=[any_spec, vmem_spec] + [any_spec] * 4 +...  337 us
    unnamed x1, local copies, waits for them, and re-layouts  14.1 us

profile of v2, /device:TPU:0, one launch (start us, length us, event | category | flops | bytes accessed | tf_op | source)
XLA Modules:
  0.0 356.3 jit_solution(10984193106649845928)
XLA Ops:
  0.6 0.6 maximum_bitcast_fusion.freq_ref
  1.2 336.8 %sublayer.1 = (bf16[2048,4096]{1,0:T(8,128)(2,1)}, bf16[8,256,256]{2,1,0:T(8,128)(2,1)}, bf16[2048,256]{1,0:T(8,128)(2,1)}, bf16[32,2048,128]{2,1,0:T(8,128)(2,1...) custom-call(bf16[2048,4096]{1,0:T(8,128)(2,1)} %x_ref.1, bf16[32,128]{1,0:T(8,128)(2,1)} %bitcast.3, ...), custom_call_target="tpu_custom_call" | custom-call | tf_op jit(solution)/shard_map/sublayer/pallas_call | solution.py:906
  338.0 2.1 reshape.16
  340.2 2.1 reshape.17
  342.3 14.1 %copy.11 = bf16[2048,4096]{1,0:T(8,128)(2,1)} copy(bf16[2048,4096]{1,0:T(8,128)(2,1)} %get-tuple-element.12) | data formatting | bytes 33554432
  (1 shorter events, 0.0 us)

commit v3 on v2

--- a/solution.py
+++ b/solution.py
@@ -515,13 +515,7 @@
             acc_b[...] = jnp.zeros_like(acc_b)
             n_full = g0 // bk
 
-            @pl.when(n_full > 0)
-            def _():
-                qk(0, 0)
-
-            @pl.when(n_full == 0)
-            def _():
-                qk(0, 0, k_idx <= q_idx)
+            qk(0, 0, k_idx <= q_idx + g0)
 
             def body(t):
                 qk(1, t)
@@ -531,20 +525,28 @@
 
             repeat(n_full - 1, body)
 
+            def finish_unit(tail):
+                if tail:
+                    qk(1, n_full - 1)
+                    soft(0, n_full - 1)
+                    qk(0, n_full, k_idx <= q_idx)
+                    soft(1, n_full - 1)
+                qk(1, n_full, k_idx <= q_idx + bq)
+                soft(0, n_full)
+                soft(1, n_full)
+                for st in range(2):
+                    o = accs[st][...] * (1.0 / l_run[st])
+                    for j in range(group):
+                        qb[hl * group + j, pl.ds(r0 + st * bq, bq), :] = o[:, j * bq:(j + 1) * bq].T.astype(BF16)
+
             @pl.when(n_full > 0)
             def _():
-                qk(1, n_full - 1)
-                soft(0, n_full - 1)
-                qk(0, n_full, k_idx <= q_idx)
-                soft(1, n_full - 1)
-
-            qk(1, n_full, k_idx <= q_idx + bq)
-            soft(0, n_full)
-            soft(1, n_full)
-            for st in range(2):
-                o = accs[st][...] * (1.0 / l_run[st])
-                for j in range(group):
-                    qb[hl * group + j, pl.ds(r0 + st * bq, bq), :] = o[:, j * bq:(j + 1) * bq].T.astype(BF16)
+                finish_unit(True)
+
+            @pl.when(n_full == 0)
+            def _():
+                finish_unit(False)
+
             for st in range(2):
                 rb = half * half_blk + c * 2 + st
 
@@ -618,10 +620,10 @@
 
         def after_k():
             w_stage3(MID)
+            w_stage3(END)
             w_stage4(PARTNER)
 
         def after_l():
-            w_stage3(END)
             w_stage4(MID)
             w_stage4(END)
 
@@ -938,7 +940,39 @@
         compiler_params=pltpu.CompilerParams(collective_id=0, has_side_effects=True, vmem_limit_bytes=67043328),
         name="sublayer",
     )(x, gain, w_q, w_k, w_v, w_o, positions, freqs)
-    return outs[0], outs[1], outs[2]
+    return outs[:3]
+
+
+def results(y):
+    rows, width = y.shape
+    n = 8
+    blk = rows // n
+
+    def kernel(y_in, y_out, buf, sems):
+        def copy_in(i):
+            return pltpu.make_async_copy(y_in.at[pl.ds(i * blk, blk), :], buf.at[pl.ds(i * blk, blk), :], sems.at[0, i])
+
+        def copy_out(i):
+            return pltpu.make_async_copy(buf.at[pl.ds(i * blk, blk), :], y_out.at[pl.ds(i * blk, blk), :], sems.at[1, i])
+
+        for i in range(n):
+            copy_in(i).start()
+        for i in range(n):
+            copy_in(i).wait()
+            copy_out(i).start()
+        for i in range(n):
+            copy_out(i).wait()
+
+    any_spec = pl.BlockSpec(memory_space=pl.ANY)
+    return pl.pallas_call(
+        kernel,
+        in_specs=[any_spec],
+        out_specs=any_spec,
+        out_shape=jax.ShapeDtypeStruct(y.shape, BF16),
+        scratch_shapes=[pltpu.VMEM(y.shape, BF16), pltpu.SemaphoreType.DMA((2, n))],
+        compiler_params=pltpu.CompilerParams(vmem_limit_bytes=60 * 2 ** 20),
+        name="results",
+    )(y)
 
 
 def solution(mesh):
@@ -949,7 +983,7 @@
         gain = norm_gain.reshape(-1, HEAD_DIM)
         y, keys, values = layer(x_in, gain, w_q, w_k, w_v, w_o, positions, freqs)
         shape = (x_in.shape[0], kv_heads, HEAD_DIM)
-        return y, keys.reshape(shape), values.reshape(shape)
+        return results(y), keys.reshape(shape), values.reshape(shape)
 
     row_spec = P(('dp', 'cp'), None)
     cache_spec = P(('dp', 'cp'), 'tp', None)

time: 357 us -> 351 us (0.983); the launches traced: 356 us -> 345 us
  local copies, waits for them, and re-layouts: 18.3 us -> 2.21 us
  Pallas kernels: 337 us -> 341 us
    unnamed x1 -> x4, local copies, waits for them, and re-layouts: 14.1 us -> 0.01 us
    pallas_call x0 -> x1, Pallas kernels: none -> 12 us  [results(): pl.pallas_call(kernel, in_specs=[any_spec], out_specs=any_spec, out_shape...]
    pallas_call x1, Pallas kernels: 337 us -> 329 us  [layer(): pl.pallas_call(kernel, in_specs=[any_spec, vmem_spec] + [any_spec] * 4 +...]
where the time goes in v3:
time: 351 us; the launch traced here: 345 us
  Pallas kernels  341 us (97%)
    pallas_call x1, Pallas kernels, layer(): pl.pallas_call(kernel, in_specs=[any_spec, vmem_spec] + [any_spec] * 4 +...  329 us
    pallas_call x1, Pallas kernels, results(): pl.pallas_call(kernel, in_specs=[any_spec], out_specs=any_spec, out_shape...  12 us

profile of v3, /device:TPU:0, one launch (start us, length us, event | category | flops | bytes accessed | tf_op | source)
XLA Modules:
  0.0 344.9 jit_solution(11055105261226986675)
XLA Ops:
  0.6 0.6 maximum_bitcast_fusion.freq_ref
  1.2 329.5 %sublayer.1 = (bf16[2048,4096]{1,0:T(8,128)(2,1)}, bf16[8,256,256]{2,1,0:T(8,128)(2,1)}, bf16[2048,256]{1,0:T(8,128)(2,1)}, bf16[32,2048,128]{2,1,0:T(8,128)(2,1...) custom-call(bf16[2048,4096]{1,0:T(8,128)(2,1)} %x_ref.1, bf16[32,128]{1,0:T(8,128)(2,1)} %bitcast.3, ...), custom_call_target="tpu_custom_call" | custom-call | tf_op jit(solution)/shard_map/sublayer/pallas_call | solution.py:908
  330.7 0.0 copy-start.1
  330.7 0.0 copy-start
  330.8 12.0 %results.1 = bf16[2048,4096]{1,0:T(8,128)(2,1)} custom-call(bf16[2048,4096]{1,0:T(8,128)(2,1)} %get-tuple-element.6.y_in), custom_call_target="tpu_custom_call" | custom-call | tf_op jit(solution)/shard_map/results/pallas_call | solution.py:967
  342.7 0.0 copy-done.1
  342.7 1.1 reshape.16
  343.8 0.0 copy-done
  343.8 1.1 reshape.17
  (1 shorter events, 0.0 us)
Async XLA Ops:
  330.7 12.0 %copy-start.1 = (bf16[8,256,256]{2,1,0:T(8,128)(2,1)S(1)}, bf16[8,256,256]{2,1,0:T(8,128)(2,1)}, u32[]{:S(2)}) copy-start(bf16[8,256,256]{2,1,0:T(8,128)(2,1)} %get-tuple-element.7) | copy-start | bytes 3145732
  330.7 13.1 %copy-start = (bf16[2048,256]{1,0:T(8,128)(2,1)S(1)}, bf16[2048,256]{1,0:T(8,128)(2,1)}, u32[]{:S(2)}) copy-start(bf16[2048,256]{1,0:T(8,128)(2,1)} %get-tuple-element.8) | copy-start | bytes 3145732

commit v4 on v3

--- a/solution.py
+++ b/solution.py
@@ -110,11 +110,6 @@
         def at_rows(n, size):
             return pl.ds(pl.multiple_of(n, size), size)
 
-        barrier = pltpu.get_barrier_semaphore()
-        for dev in (x_nb, y_nb, c_nb, {"tp": partner}, {"tp": other_mid}, {"tp": other_end}):
-            pl.semaphore_signal(barrier, inc=1, device_id=dev, device_id_type=MESH)
-        pl.semaphore_wait(barrier, 6)
-
         place = dp * 4 + cp
 
         def place_of(fx, fy, fc):
@@ -256,6 +251,11 @@
         load_k.start()
         load_v.start()
         load_q.start()
+
+        barrier = pltpu.get_barrier_semaphore()
+        for dev in (x_nb, y_nb, c_nb, {"tp": partner}, {"tp": other_mid}, {"tp": other_end}):
+            pl.semaphore_signal(barrier, inc=1, device_id=dev, device_id_type=MESH)
+        pl.semaphore_wait(barrier, 6)
 
         @pl.when(middle)
         def _():

time: 351 us -> 348 us (level)
  no operation moved by 1% of the time
where the time goes in v4:
time: 348 us; the launch traced here: 343 us
  Pallas kernels  340 us (98%)
    pallas_call x1, Pallas kernels, layer(): pl.pallas_call(kernel, in_specs=[any_spec, vmem_spec] + [any_spec] * 4 +...  328 us
    pallas_call x1, Pallas kernels, results(): pl.pallas_call(kernel, in_specs=[any_spec], out_specs=any_spec, out_shape...  12 us

profile of v4, /device:TPU:0, one launch (start us, length us, event | category | flops | bytes accessed | tf_op | source)
XLA Modules:
  0.0 343.5 jit_solution(17033658782215892992)
XLA Ops:
  0.6 0.6 maximum_bitcast_fusion.freq_ref
  1.2 328.0 %sublayer.1 = (bf16[2048,4096]{1,0:T(8,128)(2,1)}, bf16[8,256,256]{2,1,0:T(8,128)(2,1)}, bf16[2048,256]{1,0:T(8,128)(2,1)}, bf16[32,2048,128]{2,1,0:T(8,128)(2,1...) custom-call(bf16[2048,4096]{1,0:T(8,128)(2,1)} %x_ref.1, bf16[32,128]{1,0:T(8,128)(2,1)} %bitcast.3, ...), custom_call_target="tpu_custom_call" | custom-call | tf_op jit(solution)/shard_map/sublayer/pallas_call | solution.py:908
  329.3 0.0 copy-start.1
  329.3 0.0 copy-start
  329.3 12.0 %results.1 = bf16[2048,4096]{1,0:T(8,128)(2,1)} custom-call(bf16[2048,4096]{1,0:T(8,128)(2,1)} %get-tuple-element.6.y_in), custom_call_target="tpu_custom_call" | custom-call | tf_op jit(solution)/shard_map/results/pallas_call | solution.py:967
  341.2 0.0 copy-done.1
  341.2 1.1 reshape.16
  342.4 0.0 copy-done
  342.4 1.1 reshape.17
  (1 shorter events, 0.0 us)
Async XLA Ops:
  329.3 12.0 %copy-start.1 = (bf16[8,256,256]{2,1,0:T(8,128)(2,1)S(1)}, bf16[8,256,256]{2,1,0:T(8,128)(2,1)}, u32[]{:S(2)}) copy-start(bf16[8,256,256]{2,1,0:T(8,128)(2,1)} %get-tuple-element.7) | copy-start | bytes 3145732
  329.3 13.1 %copy-start = (bf16[2048,256]{1,0:T(8,128)(2,1)S(1)}, bf16[2048,256]{1,0:T(8,128)(2,1)}, u32[]{:S(2)}) copy-start(bf16[2048,256]{1,0:T(8,128)(2,1)} %get-tuple-element.8) | copy-start | bytes 3145732

commit v5 on v4

--- a/solution.py
+++ b/solution.py
@@ -622,9 +622,9 @@
             w_stage3(MID)
             w_stage3(END)
             w_stage4(PARTNER)
+            w_stage4(MID)
 
         def after_l():
-            w_stage4(MID)
             w_stage4(END)
 
         end_units = (

time: 348 us -> 350 us (level); the launches traced: 343 us -> 350 us
  Pallas kernels: 340 us -> 347 us
    pallas_call x1, Pallas kernels: 328 us -> 335 us  [layer(): pl.pallas_call(kernel, in_specs=[any_spec, vmem_spec] + [any_spec] * 4 +...]
where the time goes in v5:
time: 350 us
  Pallas kernels  347 us (99%)
    pallas_call x1, Pallas kernels, layer(): pl.pallas_call(kernel, in_specs=[any_spec, vmem_spec] + [any_spec] * 4 +...  335 us
    pallas_call x1, Pallas kernels, results(): pl.pallas_call(kernel, in_specs=[any_spec], out_specs=any_spec, out_shape...  12 us

profile of v5, /device:TPU:0, one launch (start us, length us, event | category | flops | bytes accessed | tf_op | source)
XLA Modules:
  0.0 350.0 jit_solution(13899495765445452129)
XLA Ops:
  0.6 0.6 maximum_bitcast_fusion.freq_ref
  1.2 334.6 %sublayer.1 = (bf16[2048,4096]{1,0:T(8,128)(2,1)}, bf16[8,256,256]{2,1,0:T(8,128)(2,1)}, bf16[2048,256]{1,0:T(8,128)(2,1)}, bf16[32,2048,128]{2,1,0:T(8,128)(2,1...) custom-call(bf16[2048,4096]{1,0:T(8,128)(2,1)} %x_ref.1, bf16[32,128]{1,0:T(8,128)(2,1)} %bitcast.3, ...), custom_call_target="tpu_custom_call" | custom-call | tf_op jit(solution)/shard_map/sublayer/pallas_call | solution.py:908
  335.8 0.0 copy-start.1
  335.8 0.0 copy-start
  335.8 12.0 %results.1 = bf16[2048,4096]{1,0:T(8,128)(2,1)} custom-call(bf16[2048,4096]{1,0:T(8,128)(2,1)} %get-tuple-element.6.y_in), custom_call_target="tpu_custom_call" | custom-call | tf_op jit(solution)/shard_map/results/pallas_call | solution.py:967
  347.8 0.0 copy-done.1
  347.8 1.1 reshape.16
  348.9 0.0 copy-done
  348.9 1.1 reshape.17
  (1 shorter events, 0.0 us)
Async XLA Ops:
  335.8 12.0 %copy-start.1 = (bf16[8,256,256]{2,1,0:T(8,128)(2,1)S(1)}, bf16[8,256,256]{2,1,0:T(8,128)(2,1)}, u32[]{:S(2)}) copy-start(bf16[8,256,256]{2,1,0:T(8,128)(2,1)} %get-tuple-element.7) | copy-start | bytes 3145732
  335.8 13.1 %copy-start = (bf16[2048,256]{1,0:T(8,128)(2,1)S(1)}, bf16[2048,256]{1,0:T(8,128)(2,1)}, u32[]{:S(2)}) copy-start(bf16[2048,256]{1,0:T(8,128)(2,1)} %get-tuple-element.8) | copy-start | bytes 3145732
